TPU v7x, 256 devices: a whole 4x4x8 slice. The times are simulated.
256 devices in a mesh: seq: 64 (over x, y, z_lo), tensor: 4 (over z_hi, core).
Axes of the slice: x: 4, y: 4, z: 8 (z_hi: 2, z_lo: 4; z = z_hi * 4 + z_lo), core: 2. Of those that a mesh axis runs over, the one named last changes fastest.
Arguments:
- queries: bfloat16 [8192, 4096], P(('seq', 'tensor')), may hold values from -5 to 5
- keys: bfloat16 [8192, 1024], P(('seq', 'tensor')), may hold values from -5 to 5
- values: bfloat16 [8192, 1024], P(('seq', 'tensor')), may hold values from -5 to 5
- mamba_x: bfloat16 [8192, 8192], P(('seq', 'tensor')), may hold values from -5 to 5
- mamba_b: bfloat16 [8192, 1024], P(('seq', 'tensor')), may hold values from -5 to 5
- mamba_c: bfloat16 [8192, 1024], P(('seq', 'tensor')), may hold values from -5 to 5
- mamba_dt: bfloat16 [8192, 128], P(('seq', 'tensor')), may hold values from -4 to 4
- conv_x: bfloat16 [4, 8192], P(None, 'tensor'), may hold values from -3 to 3
- conv_b: bfloat16 [4, 1024], P(None, 'tensor'), may hold values from -3 to 3
- conv_c: bfloat16 [4, 1024], P(None, 'tensor'), may hold values from -3 to 3
- dt_bias: float32 [128], P('tensor'), may hold values from -1 to 1
- decay_rate: float32 [128], P('tensor'), may hold values from 0.0001 to 0.05
- skip_gain: float32 [128], P('tensor'), may hold values from 0.5 to 1.5
- norm_gain: float32 [8192], P('tensor'), may hold values from 0.5 to 1.5
- windows: int32 [32], replicated, may hold values from 1056 to 4224, as said below
- doc_lengths: int32 [3], replicated, may hold values from 1 to 6144, 8192 in all
Outputs:
- attn_out: bfloat16 [8192, 4096], P('seq', 'tensor')
- mamba_out: bfloat16 [8192, 8192], P('seq', 'tensor')
- attn_checksum: float32 [4096], P('tensor')
- mamba_checksum: float32 [8192], P('tensor')
Inputs may be any that keep to these rules, and one draw needn't show every extreme that they name: `windows`: one of the 32 query heads has a window of exactly 4224 tokens. `doc_lengths`: 3 lengths summing to 8192; the longest is exactly three quarters of 8192.
All inputs are finite; a program needn't handle non-finite values.
Results may differ from a plain program's by a relative error of at most 0.007.
Values may be sent and summed in bfloat16 or wider, within the bound.
A program may use at most 192 MiB of HBM per device.

v0:
```python
import math

import jax
import jax.numpy as jnp
from jax import lax
from jax.sharding import Mesh
from jax.sharding import PartitionSpec as P

HEAD_SIZE = 128
MP = 64
MN = 128
KC = 4
SEQ = ("seq_0", "seq_1", "seq_2")
SEQ_TENSOR = ("seq_0", "seq_1", "seq_2", "tensor")


NEG_LARGE = -1e30
EPS_NORM = 1e-05


def shifted(block, axis, distance):
    devices = range(lax.axis_size(axis))
    route = [(i - distance, i) for i in devices if i - distance in devices]
    return lax.ppermute(block, axis, route)


def nothing_yet(x, identity):
    return jax.tree.map(
        lambda a, e: jnp.broadcast_to(jnp.asarray(e, a.dtype), a.shape), x, identity
    )


def entering_2(x, axes, combine, identity):
    before = start = nothing_yet(x, identity)
    subtotal = x
    for axis in reversed(axes):
        length, here = (lax.axis_size(axis), lax.axis_index(axis))
        pieces = jax.tree.map(
            lambda part, kind: lax.all_gather(part.astype(kind), axis),
            subtotal,
            (jnp.bfloat16, jnp.bfloat16),
        )
        inside, subtotal = (start, start)
        for k in range(length):
            passed = k < here
            subtotal = combine(
                subtotal, jax.tree.map(lambda part, own: part[k].astype(own.dtype), pieces, x)
            )
            inside = jax.tree.map(lambda new, old: jnp.where(passed, new, old), subtotal, inside)
        before = combine(inside, before)
    return before


def copy_for_each(x, axis):
    copies = jnp.broadcast_to(x, (lax.axis_size(axis), *x.shape))
    return lax.all_to_all(copies, axis, split_axis=0, concat_axis=0, tiled=True)


def over_copies(x, axis):
    everything = copy_for_each(x, axis)
    return jnp.sum(everything, axis=0)


def in_one(arrays, axis):
    vector, at, outs = (jnp.concatenate([a.reshape(-1) for a in arrays]), 0, [])
    subtotal = over_copies(vector, axis)
    for a in arrays:
        outs.append(subtotal[at : at + a.size].reshape(a.shape))
        at += a.size
    return tuple(outs)


def doc_table(doc_lengths):
    return jnp.cumsum(doc_lengths) - doc_lengths


def doc_index(positions, doc_starts):
    return jnp.sum((positions[:, None] >= doc_starts[None, :]).astype(jnp.int32), axis=1) - 1


def allowed_mask(query_pos, key_pos, doc_starts, window_per_head):
    gap = query_pos[:, None] - key_pos[None, :]
    same_doc = doc_index(query_pos, doc_starts)[:, None] == doc_index(key_pos, doc_starts)[None, :]
    base_ok = (gap >= 0) & (key_pos[None, :] >= 0) & same_doc
    return base_ok[None, None] & (gap[None, None] < window_per_head[:, :, None, None])


def attend_piece(
    carry, piece, key_start, grouped_heads, query_pos, doc_starts, window_per_head, reach
):
    key_rows, value_rows = piece
    key_count = key_rows.shape[0]
    shared_heads = grouped_heads.shape[1]
    key_pos = key_start + jnp.arange(key_count, dtype=jnp.int32)

    def compute(state):
        old_max, old_total, old_accum = state
        keys_rank3 = key_rows.reshape(key_count, shared_heads, HEAD_SIZE)
        values_rank3 = value_rows.reshape(key_count, shared_heads, HEAD_SIZE)
        scores = jnp.einsum(
            "tgqd,sgd->gqts", grouped_heads, keys_rank3, preferred_element_type=jnp.float32
        ) * (1.0 / math.sqrt(HEAD_SIZE))
        allowed = allowed_mask(query_pos, key_pos, doc_starts, window_per_head)
        scores = jnp.where(allowed, scores, NEG_LARGE)
        new_max = jnp.maximum(old_max, jnp.max(scores, axis=-1))
        weights = jnp.where(allowed, jnp.exp(scores - new_max[..., None]), 0.0)
        rescale = jnp.exp(old_max - new_max)
        new_total = old_total * rescale + jnp.sum(weights, axis=-1)
        product = jnp.einsum(
            "gqts,sgd->gqtd",
            weights.astype(jnp.bfloat16),
            values_rank3,
            preferred_element_type=jnp.float32,
        )
        return (new_max, new_total, old_accum * rescale[..., None] + product)

    touches = (key_start + key_count - 1 >= query_pos[0] - reach) & (key_start <= query_pos[-1])
    return lax.cond(touches, compute, lambda state: state, carry)


def causal_conv(extended, taps, positions, doc_starts):
    count = positions.shape[0]
    docs_out = doc_index(positions, doc_starts)
    ext_pos = positions[0] - (KC - 1) + jnp.arange(count + KC - 1, dtype=jnp.int32)
    docs_ext = doc_index(ext_pos, doc_starts)
    running = jnp.zeros((count, extended.shape[1]), jnp.float32)
    for tap_index in range(KC):
        offset = KC - 1 - tap_index
        valid = (docs_ext[offset : offset + count] == docs_out) & (
            ext_pos[offset : offset + count] >= 0
        )
        term = taps[tap_index].astype(jnp.float32)[None, :] * extended[
            offset : offset + count
        ].astype(jnp.float32)
        running = running + jnp.where(valid[:, None], term, 0.0)
    return jax.nn.silu(running).astype(jnp.bfloat16)


def stretch_terms(x_rows, b_rows, c_rows, dt_rows, positions, doc_starts, dt_bias, decay_rate):
    count = positions.shape[0]
    heads = x_rows.shape[1] // MP
    groups = b_rows.shape[1] // MN
    per_group = heads // groups
    docs = doc_index(positions, doc_starts)
    prior_doc = doc_index(positions[:1] - 1, doc_starts)[0]
    delta = jax.nn.softplus(dt_rows.astype(jnp.float32) + dt_bias[None, :])
    log_decay = -delta * decay_rate[None, :]
    running = jnp.cumsum(log_decay, axis=0)
    running_heads = running.T
    order = jnp.arange(count, dtype=jnp.int32)
    causal = order[:, None] >= order[None, :]
    same_doc = docs[:, None] == docs[None, :]
    gaps = running_heads[:, :, None] - running_heads[:, None, :]
    segment = jnp.where((causal & same_doc)[None], jnp.exp(jnp.minimum(gaps, 0.0)), 0.0)
    inputs3 = x_rows.reshape(count, heads, MP)
    b_groups = b_rows.reshape(count, groups, MN)
    c_groups = c_rows.reshape(count, groups, MN)
    cross = jnp.einsum("tgn,sgn->gts", c_groups, b_groups, preferred_element_type=jnp.float32)
    cross_heads = jnp.repeat(cross, per_group, axis=0)
    mixing = (segment * cross_heads * delta.T[:, None, :]).astype(jnp.bfloat16)
    intra = jnp.einsum("hts,shp->thp", mixing, inputs3, preferred_element_type=jnp.float32)
    last_doc = docs[count - 1]
    to_end = (
        jnp.where((docs == last_doc)[:, None], jnp.exp(running[count - 1][None, :] - running), 0.0)
        * delta
    )
    weighted = (inputs3.astype(jnp.float32) * to_end[:, :, None]).astype(jnp.bfloat16)
    b_heads = jnp.repeat(b_groups, per_group, axis=1)
    local_state = jnp.einsum("shp,shn->hpn", weighted, b_heads, preferred_element_type=jnp.float32)
    carry_factor = jnp.where(prior_doc == last_doc, jnp.exp(running[count - 1]), 0.0)
    inflow = jnp.where((docs == prior_doc)[:, None], jnp.exp(running), 0.0)
    c_heads = jnp.repeat(c_groups, per_group, axis=1)
    return (intra, local_state, carry_factor, inflow, c_heads)


def stretch_finish(intra, incoming, inflow, c_heads, x_rows, skip_gain, norm_gain):
    count = x_rows.shape[0]
    heads = x_rows.shape[1] // MP
    incoming_bf = incoming.astype(jnp.bfloat16)
    entering = (
        jnp.einsum("thn,hpn->thp", c_heads, incoming_bf, preferred_element_type=jnp.float32)
        * inflow[:, :, None]
    )
    inputs3 = x_rows.reshape(count, heads, MP).astype(jnp.float32)
    mixed = intra + entering + skip_gain[None, :, None] * inputs3
    mean_square = jnp.mean(mixed * mixed, axis=-1, keepdims=True)
    normed = mixed * lax.rsqrt(mean_square + EPS_NORM) * norm_gain.reshape(heads, MP)[None]
    return normed.reshape(count, heads * MP).astype(jnp.bfloat16)


def combine_states(earlier, later):
    return (earlier[0] * later[0], later[0][:, None, None] * earlier[1] + later[1])


def local(
    queries,
    keys,
    values,
    mamba_x,
    mamba_b,
    mamba_c,
    mamba_dt,
    conv_x,
    conv_b,
    conv_c,
    dt_bias,
    decay_rate,
    skip_gain,
    norm_gain,
    windows,
    doc_lengths,
):
    served = (
        lax.all_to_all(queries, "tensor", split_axis=1, concat_axis=0, tiled=True),
        lax.all_to_all(keys, "tensor", split_axis=1, concat_axis=0, tiled=True),
        lax.all_to_all(values, "tensor", split_axis=1, concat_axis=0, tiled=True),
        lax.all_to_all(mamba_x, "tensor", split_axis=1, concat_axis=0, tiled=True),
        lax.all_to_all(mamba_b, "tensor", split_axis=1, concat_axis=0, tiled=True),
        lax.all_to_all(mamba_c, "tensor", split_axis=1, concat_axis=0, tiled=True),
        lax.all_to_all(mamba_dt, "tensor", split_axis=1, concat_axis=0, tiled=True),
    )
    query_rows, key_rows, value_rows, x_rows, b_rows, c_rows, dt_rows = served
    row_count = query_rows.shape[0]
    shard_start = lax.axis_index(SEQ) * row_count
    positions = shard_start + jnp.arange(row_count, dtype=jnp.int32)
    doc_starts = doc_table(doc_lengths)
    query_heads = query_rows.shape[1] // HEAD_SIZE
    shared_heads = key_rows.shape[1] // HEAD_SIZE
    group_width = query_heads // shared_heads
    window_per_head = lax.dynamic_slice_in_dim(
        windows, lax.axis_index("tensor") * query_heads, query_heads
    ).reshape(shared_heads, group_width)
    reach = jnp.max(window_per_head)
    grouped_heads = query_rows.reshape(row_count, shared_heads, group_width, HEAD_SIZE)
    initial = (
        jnp.full((shared_heads, group_width, row_count), NEG_LARGE, jnp.float32),
        jnp.zeros((shared_heads, group_width, row_count), jnp.float32),
        jnp.zeros((shared_heads, group_width, row_count, HEAD_SIZE), jnp.float32),
    )

    def attend(carry, piece, key_start):
        return attend_piece(
            carry, piece, key_start, grouped_heads, positions, doc_starts, window_per_head, reach
        )

    span = lax.axis_size(SEQ) // 2 + 1
    earlier = shifted((key_rows, value_rows), SEQ, 1)
    held_keys, held_values = earlier
    for level in range((span - 1).bit_length()):
        farther = shifted((held_keys, held_values), SEQ, 1 << level)
        held_keys = jnp.concatenate([farther[0], held_keys], axis=0)
        held_values = jnp.concatenate([farther[1], held_values], axis=0)
    held_keys = held_keys[held_keys.shape[0] - span * row_count :]
    held_values = held_values[held_values.shape[0] - span * row_count :]
    per_block = math.gcd(span, max(1, 1024 // row_count))
    block_rows = per_block * row_count
    block_count = span // per_block
    stacked_keys = held_keys.reshape(block_count, block_rows, held_keys.shape[1])
    stacked_values = held_values.reshape(block_count, block_rows, held_values.shape[1])
    first_key = shard_start - span * row_count

    def sweep(carry, inputs):
        block_keys, block_values, block_number = inputs
        return (
            attend(carry, (block_keys, block_values), first_key + block_number * block_rows),
            None,
        )

    final, unused_out = lax.scan(
        sweep, initial, (stacked_keys, stacked_values, jnp.arange(block_count, dtype=jnp.int32))
    )
    final = attend(final, (key_rows, value_rows), shard_start)
    final_max, totals, accum = final
    attention = (
        (accum / totals[..., None])
        .transpose(2, 0, 1, 3)
        .reshape(row_count, query_heads * HEAD_SIZE)
        .astype(jnp.bfloat16)
    )
    edge = row_count - (KC - 1)
    tails = shifted((x_rows[edge:], b_rows[edge:], c_rows[edge:]), SEQ, 1)
    conv_x_out = causal_conv(
        jnp.concatenate([tails[0], x_rows], axis=0), conv_x, positions, doc_starts
    )
    conv_b_out = causal_conv(
        jnp.concatenate([tails[1], b_rows], axis=0), conv_b, positions, doc_starts
    )
    conv_c_out = causal_conv(
        jnp.concatenate([tails[2], c_rows], axis=0), conv_c, positions, doc_starts
    )
    intra, local_state, carry_factor, inflow, c_heads = stretch_terms(
        conv_x_out, conv_b_out, conv_c_out, dt_rows, positions, doc_starts, dt_bias, decay_rate
    )
    incoming = entering_2(
        (carry_factor, local_state),
        SEQ,
        combine_states,
        (jnp.ones_like(carry_factor), jnp.zeros_like(local_state)),
    )
    mamba_out = stretch_finish(
        intra, incoming[1], inflow, c_heads, conv_x_out, skip_gain, norm_gain
    )
    sums = in_one(
        (
            jnp.sum(attention.astype(jnp.float32), axis=0),
            jnp.sum(mamba_out.astype(jnp.float32), axis=0),
        ),
        SEQ,
    )
    return (attention, mamba_out, sums[0], sums[1])


def solution(mesh):
    torus = Mesh(
        mesh.devices.reshape(4, 4, 4, mesh.shape["tensor"]), ("seq_0", "seq_1", "seq_2", "tensor")
    )
    in_specs = (
        P(SEQ_TENSOR, None),
        P(SEQ_TENSOR, None),
        P(SEQ_TENSOR, None),
        P(SEQ_TENSOR, None),
        P(SEQ_TENSOR, None),
        P(SEQ_TENSOR, None),
        P(SEQ_TENSOR, None),
        P(None, "tensor"),
        P(None, "tensor"),
        P(None, "tensor"),
        P("tensor"),
        P("tensor"),
        P("tensor"),
        P("tensor"),
        P(),
        P(),
    )
    out_specs = (P(SEQ, "tensor"), P(SEQ, "tensor"), P("tensor"), P("tensor"))
    return jax.shard_map(local, mesh=torus, in_specs=in_specs, out_specs=out_specs, check_vma=False)
```

profile of v0, /device:TPU:128, one launch (start us, length us, event | category | flops | bytes accessed | tf_op | source)
XLA Modules:
  0.0 537.8 jit_solution(2503243864806714824)
XLA Ops:
  8.7 7.2 %all-to-all-start.4 = ((bf16[4,2,512]{2,1,0:T(2,128)(2,1)}), bf16[4,2,512]{2,1,0:T(2,128)(2,1)S(1)}, u32[]{:S(2)}, u32[]{:S(2)}) async-start(bf16[4,2,512]{2,1,0:T(2,128)(2,1)} %reshape.771), calls=%async_computation.4 | async-start | bytes 16384 | tf_op jit(solution)/shard_map/all_to_all | solution.py:220
  23.3 7.2 %all-to-all-start.6 = ((bf16[32,4,256]{2,0,1:T(8,128)(2,1)}), bf16[32,4,256]{2,0,1:T(8,128)(2,1)S(1)}, u32[]{:S(2)}, u32[]{:S(2)}) async-start(bf16[32,4,256]{2,0,1:T(8,128)(2,1)} %bitcast.337), calls=%async_computation.6 | async-start | bytes 131072 | tf_op jit(solution)/shard_map/all_to_all | solution.py:218
  33.7 8.3 %all-to-all-start.3 = ((bf16[32,4,2048]{2,0,1:T(8,128)(2,1)}), bf16[32,4,2048]{2,0,1:T(8,128)(2,1)S(1)}, u32[]{:S(2)}, u32[]{:S(2)}) async-start(bf16[32,4,2048]{2,0,1:T(8,128)(2,1)} %bitcast.335), calls=%async_computation.3 | async-start | bytes 1048576 | tf_op jit(solution)/shard_map/all_to_all | solution.py:217
  50.4 7.6 %collective-permute-start.14 = (bf16[3,2048]{1,0:T(4,128)(2,1)S(1)}, bf16[3,2048]{1,0:T(4,128)(2,1)S(1)}, u32[]{:S(2)}, u32[]{:S(2)}) collective-permute-start(bf16[3,2048]{1,0:T(4,128)(2,1)S(1)} %slice.307), channel_id=1, source_target_pairs={{0,4},{4,8},{8,12},{12,16},{16,20},{20,24},{24,28},{28,32},{32,36}... | collective-permute-start | bytes 36872 | tf_op jit(solution)/shard_map/ppermute | solution.py:24
  62.9 8.6 %all-to-all-start.2 = ((bf16[32,4,256]{2,0,1:T(8,128)(2,1)}), bf16[32,4,256]{2,0,1:T(8,128)(2,1)S(1)}, u32[]{:S(2)}, u32[]{:S(2)}) async-start(bf16[32,4,256]{2,0,1:T(8,128)(2,1)} %bitcast.339), calls=%async_computation.2 | async-start | bytes 131072 | tf_op jit(solution)/shard_map/all_to_all | solution.py:216
  73.9 9.6 %all-to-all-start = ((bf16[32,4,256]{2,0,1:T(8,128)(2,1)}), bf16[32,4,256]{2,0,1:T(8,128)(2,1)S(1)}, u32[]{:S(2)}, u32[]{:S(2)}) async-start(bf16[32,4,256]{2,0,1:T(8,128)(2,1)} %bitcast.340), calls=%async_computation | async-start | bytes 131072 | tf_op jit(solution)/shard_map/all_to_all | solution.py:215
  88.4 8.1 %all-to-all-start.5 = ((bf16[32,4,256]{2,0,1:T(8,128)(2,1)}), bf16[32,4,256]{2,0,1:T(8,128)(2,1)}, u32[]{:S(2)}, u32[]{:S(2)}) async-start(bf16[32,4,256]{2,0,1:T(8,128)(2,1)} %bitcast.338), calls=%async_computation.5 | async-start | bytes 131072 | tf_op jit(solution)/shard_map/all_to_all | solution.py:219
  96.5 4.9 collective-permute-start
  108.6 11.9 %all-gather.1 = bf16[4,1,32]{2,1,0:T(2,128)(2,1)S(1)} all-gather(bf16[1,1,32]{2,1,0:T(2,128)(2,1)S(1)} %get-tuple-element.613), channel_id=1, replica_groups=mesh['seq_0'=4,'seq_1'=4,'seq_2'=4,'tensor'=4] {'seq_2'}, dimensions={0}, use_global_device_ids=true | all-gather | bytes 320 | tf_op jit(solution)/shard_map/all_gather | solution.py:39
  124.6 9.6 %all-gather.2 = bf16[4,1,32]{2,1,0:T(2,128)(2,1)S(1)} all-gather(bf16[1,1,32]{2,1,0:T(2,128)(2,1)S(1)} %fusion.98), channel_id=1, replica_groups=mesh['seq_0'=4,'seq_1'=4,'seq_2'=4,'tensor'=4] {'seq_1'}, dimensions={0}, use_global_device_ids=true | all-gather | bytes 320 | tf_op jit(solution)/shard_map/all_gather | solution.py:39
  134.2 5.6 %collective-permute-start.2 = (bf16[256,256]{1,0:T(8,128)(2,1)S(1)}, bf16[256,256]{1,0:T(8,128)(2,1)S(1)}, u32[]{:S(2)}, u32[]{:S(2)}) collective-permute-start(bf16[256,256]{1,0:T(8,128)(2,1)S(1)} %pad_maximum_fusion.5), channel_id=1, source_target_pairs={{0,8},{4,12},{8,16},{12,20},{16,24},{20,28},{24,32},{28,36},{32,40... | collective-permute-start | bytes 393224 | tf_op jit(solution)/shard_map/ppermute | solution.py:24
  147.9 4.5 collective-permute-start.11
  152.4 11.7 %all-gather.3 = bf16[4,1,32]{2,1,0:T(2,128)(2,1)} all-gather(bf16[1,1,32]{2,1,0:T(2,128)(2,1)S(1)} %fusion.96), channel_id=1, replica_groups=mesh['seq_0'=4,'seq_1'=4,'seq_2'=4,'tensor'=4] {'seq_0'}, dimensions={0}, use_global_device_ids=true | all-gather | bytes 320 | tf_op jit(solution)/shard_map/all_gather | solution.py:39
  165.6 8.4 %collective-permute-start.4 = (bf16[1024,256]{1,0:T(8,128)(2,1)}, bf16[1024,256]{1,0:T(8,128)(2,1)S(1)}, u32[]{:S(2)}, u32[]{:S(2)}) collective-permute-start(bf16[1024,256]{1,0:T(8,128)(2,1)} %pad_maximum_fusion.1), channel_id=1, source_target_pairs={{0,32},{4,36},{8,40},{12,44},{16,48},{20,52},{24,56},{28,60},{32,6... | collective-permute-start | bytes 1572872 | tf_op jit(solution)/shard_map/ppermute | solution.py:24
  187.2 8.6 %collective-permute-start.5 = (bf16[2048,256]{1,0:T(8,128)(2,1)}, bf16[2048,256]{1,0:T(8,128)(2,1)}, u32[]{:S(2)}, u32[]{:S(2)}) collective-permute-start(bf16[2048,256]{1,0:T(8,128)(2,1)} %constant_dynamic-update-slice_fusion), channel_id=1, source_target_pairs={{0,64},{4,68},{8,72},{12,76},{16,80},{20,84},{24,88},{28,92},{32,9... | collective-permute-start | bytes 3145736 | tf_op jit(solution)/shard_map/ppermute | solution.py:24
  195.8 7.3 %collective-permute-done.12 = bf16[2048,256]{1,0:T(8,128)(2,1)S(1)} collective-permute-done((bf16[2048,256]{1,0:T(8,128)(2,1)}, bf16[2048,256]{1,0:T(8,128)(2,1)S(1)}, u32[]{:S(2)}, u32[]{:S(2)}) %collective-permute-start.12) | collective-permute-done | bytes 1048608 | tf_op jit(solution)/shard_map/ppermute | solution.py:24
  207.5 8.0 %collective-permute-start.13 = (bf16[4096,256]{1,0:T(8,128)(2,1)}, bf16[4096,256]{1,0:T(8,128)(2,1)}, u32[]{:S(2)}, u32[]{:S(2)}) collective-permute-start(bf16[4096,256]{1,0:T(8,128)(2,1)} %constant_dynamic-update-slice_fusion.23), channel_id=1, source_target_pairs={{0,128},{4,132},{8,136},{12,140},{16,144},{20,148},{24,152},{28,15... | collective-permute-start | bytes 6291464 | tf_op jit(solution)/shard_map/ppermute | solution.py:24
  216.2 7.2 %all-to-all-start.1 = ((bf16[32,4,1024]{2,0,1:T(8,128)(2,1)}), bf16[32,4,1024]{2,0,1:T(8,128)(2,1)}, u32[]{:S(2)}, u32[]{:S(2)}) async-start(bf16[32,4,1024]{2,0,1:T(8,128)(2,1)} %bitcast.372), calls=%async_computation.1 | async-start | bytes 524288 | tf_op jit(solution)/shard_map/all_to_all | solution.py:214
  224.6 6.2 %collective-permute-start.15 = (bf16[3,256]{1,0:T(4,128)(2,1)}, bf16[3,256]{1,0:T(4,128)(2,1)}, u32[]{:S(2)}, u32[]{:S(2)}) collective-permute-start(bf16[3,256]{1,0:T(4,128)(2,1)} %slice.312), channel_id=1, source_target_pairs={{0,4},{4,8},{8,12},{12,16},{16,20},{20,24},{24,28},{28,32},{32,36}... | collective-permute-start | bytes 4616 | tf_op jit(solution)/shard_map/ppermute | solution.py:24
  247.4 51.2 %collective-permute-start.6 = (bf16[4096,256]{1,0:T(8,128)(2,1)}, bf16[4096,256]{1,0:T(8,128)(2,1)}, u32[]{:S(2)}, u32[]{:S(2)}) collective-permute-start(bf16[4096,256]{1,0:T(8,128)(2,1)} %constant_dynamic-update-slice_fusion.5), channel_id=1, source_target_pairs={{0,128},{4,132},{8,136},{12,140},{16,144},{20,148},{24,152},{28,15... | collective-permute-start | bytes 6291464 | tf_op jit(solution)/shard_map/ppermute | solution.py:24
  315.0 6.0 %collective-permute-done.6 = bf16[4096,256]{1,0:T(8,128)(2,1)} collective-permute-done((bf16[4096,256]{1,0:T(8,128)(2,1)}, bf16[4096,256]{1,0:T(8,128)(2,1)}, u32[]{:S(2)}, u32[]{:S(2)}) %collective-permute-start.6) | collective-permute-done | bytes 2097184 | tf_op jit(solution)/shard_map/ppermute | solution.py:24
  327.1 159.9 %while.18 = (s32[]{:T(128)}, f32[2,4,128]{2,1,0:T(4,128)S(1)}, f32[2,4,128]{2,1,0:T(4,128)S(1)}, f32[2,4,128,128]{3,2,1,0:T(8,128)S(1)}, s32[33]{0:T(128)S(1)}, ...) while((s32[]{:T(128)}, f32[2,4,128]{2,1,0:T(4,128)S(1)}, ...), condition=%wide.region_9.10_spmd, body=%wide.region_2.9_spmd.sunk | while | flops 69440008 | bytes 3679539 | solution.py:269
  495.8 16.9 %all-to-all-start.7 = ((f32[64,1,3072]{2,1,0:T(1,128)}), f32[64,1,3072]{2,1,0:T(1,128)S(1)}, u32[]{:S(2)}, u32[]{:S(2)}) async-start(f32[64,1,3072]{2,1,0:T(1,128)} %broadcast_in_dim.272), calls=%async_computation.7 | async-start | bytes 1572864 | tf_op jit(solution)/shard_map/all_to_all | solution.py:56
  514.8 14.8 %all-to-all-done.7 = f32[64,1,3072]{2,1,0:T(1,128)S(1)} async-done(((f32[64,1,3072]{2,1,0:T(1,128)}), f32[64,1,3072]{2,1,0:T(1,128)S(1)}, u32[]{:S(2)}, u32[]{:S(2)}) %all-to-all-start.7) | async-done | bytes 786464 | tf_op jit(solution)/shard_map/all_to_all | solution.py:56
  (833 shorter events, 310.3 us)
Async XLA Ops:
  8.7 14.6 %all-to-all-start.4 = ((bf16[4,2,512]{2,1,0:T(2,128)(2,1)}), bf16[4,2,512]{2,1,0:T(2,128)(2,1)S(1)}, u32[]{:S(2)}, u32[]{:S(2)}) async-start(bf16[4,2,512]{2,1,0:T(2,128)(2,1)} %reshape.771), calls=%async_computation.4 | async-start | bytes 16384 | tf_op jit(solution)/shard_map/all_to_all | solution.py:220
  33.7 16.7 %all-to-all-start.3 = ((bf16[32,4,2048]{2,0,1:T(8,128)(2,1)}), bf16[32,4,2048]{2,0,1:T(8,128)(2,1)S(1)}, u32[]{:S(2)}, u32[]{:S(2)}) async-start(bf16[32,4,2048]{2,0,1:T(8,128)(2,1)} %bitcast.335), calls=%async_computation.3 | async-start | bytes 1048576 | tf_op jit(solution)/shard_map/all_to_all | solution.py:217
  42.0 137.8 %all-gather.12.cloned.1.call-start = ((), (), s32[]{:S(2)}) async-start(), calls=%async_computation.10 | async-start | bytes 2621440 | tf_op jit(solution)/shard_map/all_gather | solution.py:39
  43.8 14.2 %collective-permute-start.16 = (bf16[3,256]{1,0:T(4,128)(2,1)S(1)}, bf16[3,256]{1,0:T(4,128)(2,1)S(1)}, u32[]{:S(2)}, u32[]{:S(2)}) collective-permute-start(bf16[3,256]{1,0:T(4,128)(2,1)S(1)} %slice.317), channel_id=1, source_target_pairs={{0,4},{4,8},{8,12},{12,16},{16,20},{20,24},{24,28},{28,32},{32,36}... | collective-permute-start | bytes 4616 | tf_op jit(solution)/shard_map/ppermute | solution.py:24
  62.9 11.0 %all-to-all-start.2 = ((bf16[32,4,256]{2,0,1:T(8,128)(2,1)}), bf16[32,4,256]{2,0,1:T(8,128)(2,1)S(1)}, u32[]{:S(2)}, u32[]{:S(2)}) async-start(bf16[32,4,256]{2,0,1:T(8,128)(2,1)} %bitcast.339), calls=%async_computation.2 | async-start | bytes 131072 | tf_op jit(solution)/shard_map/all_to_all | solution.py:216
  73.9 14.5 %all-to-all-start = ((bf16[32,4,256]{2,0,1:T(8,128)(2,1)}), bf16[32,4,256]{2,0,1:T(8,128)(2,1)S(1)}, u32[]{:S(2)}, u32[]{:S(2)}) async-start(bf16[32,4,256]{2,0,1:T(8,128)(2,1)} %bitcast.340), calls=%async_computation | async-start | bytes 131072 | tf_op jit(solution)/shard_map/all_to_all | solution.py:215
  83.5 17.9 %collective-permute-start.7 = (bf16[128,256]{1,0:T(8,128)(2,1)S(1)}, bf16[128,256]{1,0:T(8,128)(2,1)S(1)}, u32[]{:S(2)}, u32[]{:S(2)}) collective-permute-start(bf16[128,256]{1,0:T(8,128)(2,1)S(1)} %bitcast.391), channel_id=1, source_target_pairs={{0,4},{4,8},{8,12},{12,16},{16,20},{20,24},{24,28},{28,32},{32,36}... | collective-permute-start | bytes 196616 | tf_op jit(solution)/shard_map/ppermute | solution.py:24
  88.4 127.7 %all-to-all-start.5 = ((bf16[32,4,256]{2,0,1:T(8,128)(2,1)}), bf16[32,4,256]{2,0,1:T(8,128)(2,1)}, u32[]{:S(2)}, u32[]{:S(2)}) async-start(bf16[32,4,256]{2,0,1:T(8,128)(2,1)} %bitcast.338), calls=%async_computation.5 | async-start | bytes 131072 | tf_op jit(solution)/shard_map/all_to_all | solution.py:219
  96.5 207.4 %all-gather.8.cloned.1.call-start = ((), (), s32[]{:S(2)}) async-start(), calls=%async_computation.8 | async-start | bytes 2621440 | tf_op jit(solution)/shard_map/all_gather | solution.py:39
  96.5 24.0 %collective-permute-start = (bf16[128,256]{1,0:T(8,128)(2,1)S(1)}, bf16[128,256]{1,0:T(8,128)(2,1)S(1)}, u32[]{:S(2)}, u32[]{:S(2)}) collective-permute-start(bf16[128,256]{1,0:T(8,128)(2,1)S(1)} %bitcast.393), channel_id=1, source_target_pairs={{0,4},{4,8},{8,12},{12,16},{16,20},{20,24},{24,28},{28,32},{32,36}... | collective-permute-start | bytes 196616 | tf_op jit(solution)/shard_map/ppermute | solution.py:24
  101.4 20.4 %collective-permute-start.8 = (bf16[128,256]{1,0:T(8,128)(2,1)S(1)}, bf16[128,256]{1,0:T(8,128)(2,1)S(1)}, u32[]{:S(2)}, u32[]{:S(2)}) collective-permute-start(bf16[128,256]{1,0:T(8,128)(2,1)S(1)} %collective-permute-done.7), channel_id=1, source_target_pairs={{0,4},{4,8},{8,12},{12,16},{16,20},{20,24},{24,28},{28,32},{32,36}... | collective-permute-start | bytes 196616 | tf_op jit(solution)/shard_map/ppermute | solution.py:24
  120.5 13.7 %collective-permute-start.1 = (bf16[128,256]{1,0:T(8,128)(2,1)S(1)}, bf16[128,256]{1,0:T(8,128)(2,1)S(1)}, u32[]{:S(2)}, u32[]{:S(2)}) collective-permute-start(bf16[128,256]{1,0:T(8,128)(2,1)S(1)} %collective-permute-done), channel_id=1, source_target_pairs={{0,4},{4,8},{8,12},{12,16},{16,20},{20,24},{24,28},{28,32},{32,36}... | collective-permute-start | bytes 196616 | tf_op jit(solution)/shard_map/ppermute | solution.py:24
  121.9 18.0 %collective-permute-start.9 = (bf16[256,256]{1,0:T(8,128)(2,1)S(1)}, bf16[256,256]{1,0:T(8,128)(2,1)S(1)}, u32[]{:S(2)}, u32[]{:S(2)}) collective-permute-start(bf16[256,256]{1,0:T(8,128)(2,1)S(1)} %pad_maximum_fusion.6), channel_id=1, source_target_pairs={{0,8},{4,12},{8,16},{12,20},{16,24},{20,28},{24,32},{28,36},{32,40... | collective-permute-start | bytes 393224 | tf_op jit(solution)/shard_map/ppermute | solution.py:24
  142.3 22.4 %collective-permute-start.3 = (bf16[512,256]{1,0:T(8,128)(2,1)S(1)}, bf16[512,256]{1,0:T(8,128)(2,1)S(1)}, u32[]{:S(2)}, u32[]{:S(2)}) collective-permute-start(bf16[512,256]{1,0:T(8,128)(2,1)S(1)} %pad_maximum_fusion.3), channel_id=1, source_target_pairs={{0,16},{4,20},{8,24},{12,28},{16,32},{20,36},{24,40},{28,44},{32,4... | collective-permute-start | bytes 786440 | tf_op jit(solution)/shard_map/ppermute | solution.py:24
  147.9 26.1 %collective-permute-start.11 = (bf16[1024,256]{1,0:T(8,128)(2,1)S(1)}, bf16[1024,256]{1,0:T(8,128)(2,1)S(1)}, u32[]{:S(2)}, u32[]{:S(2)}) collective-permute-start(bf16[1024,256]{1,0:T(8,128)(2,1)S(1)} %pad_maximum_fusion.2), channel_id=1, source_target_pairs={{0,32},{4,36},{8,40},{12,44},{16,48},{20,52},{24,56},{28,60},{32,6... | collective-permute-start | bytes 1572872 | tf_op jit(solution)/shard_map/ppermute | solution.py:24
  165.6 17.2 %collective-permute-start.4 = (bf16[1024,256]{1,0:T(8,128)(2,1)}, bf16[1024,256]{1,0:T(8,128)(2,1)S(1)}, u32[]{:S(2)}, u32[]{:S(2)}) collective-permute-start(bf16[1024,256]{1,0:T(8,128)(2,1)} %pad_maximum_fusion.1), channel_id=1, source_target_pairs={{0,32},{4,36},{8,40},{12,44},{16,48},{20,52},{24,56},{28,60},{32,6... | collective-permute-start | bytes 1572872 | tf_op jit(solution)/shard_map/ppermute | solution.py:24
  177.5 25.6 %collective-permute-start.12 = (bf16[2048,256]{1,0:T(8,128)(2,1)}, bf16[2048,256]{1,0:T(8,128)(2,1)S(1)}, u32[]{:S(2)}, u32[]{:S(2)}) collective-permute-start(bf16[2048,256]{1,0:T(8,128)(2,1)} %constant_dynamic-update-slice_fusion.18), channel_id=1, source_target_pairs={{0,64},{4,68},{8,72},{12,76},{16,80},{20,84},{24,88},{28,92},{32,9... | collective-permute-start | bytes 3145736 | tf_op jit(solution)/shard_map/ppermute | solution.py:24
  187.2 54.3 %collective-permute-start.5 = (bf16[2048,256]{1,0:T(8,128)(2,1)}, bf16[2048,256]{1,0:T(8,128)(2,1)}, u32[]{:S(2)}, u32[]{:S(2)}) collective-permute-start(bf16[2048,256]{1,0:T(8,128)(2,1)} %constant_dynamic-update-slice_fusion), channel_id=1, source_target_pairs={{0,64},{4,68},{8,72},{12,76},{16,80},{20,84},{24,88},{28,92},{32,9... | collective-permute-start | bytes 3145736 | tf_op jit(solution)/shard_map/ppermute | solution.py:24
  207.5 102.3 %collective-permute-start.13 = (bf16[4096,256]{1,0:T(8,128)(2,1)}, bf16[4096,256]{1,0:T(8,128)(2,1)}, u32[]{:S(2)}, u32[]{:S(2)}) collective-permute-start(bf16[4096,256]{1,0:T(8,128)(2,1)} %constant_dynamic-update-slice_fusion.23), channel_id=1, source_target_pairs={{0,128},{4,132},{8,136},{12,140},{16,144},{20,148},{24,152},{28,15... | collective-permute-start | bytes 6291464 | tf_op jit(solution)/shard_map/ppermute | solution.py:24
  216.2 84.2 %all-to-all-start.1 = ((bf16[32,4,1024]{2,0,1:T(8,128)(2,1)}), bf16[32,4,1024]{2,0,1:T(8,128)(2,1)}, u32[]{:S(2)}, u32[]{:S(2)}) async-start(bf16[32,4,1024]{2,0,1:T(8,128)(2,1)} %bitcast.372), calls=%async_computation.1 | async-start | bytes 524288 | tf_op jit(solution)/shard_map/all_to_all | solution.py:214
  223.4 265.6 %all-gather.10.cloned.1.call-start = ((), (), s32[]{:S(2)}) async-start(), calls=%async_computation.9 | async-start | bytes 2621440 | tf_op jit(solution)/shard_map/all_gather | solution.py:39
  224.6 11.9 %collective-permute-start.15 = (bf16[3,256]{1,0:T(4,128)(2,1)}, bf16[3,256]{1,0:T(4,128)(2,1)}, u32[]{:S(2)}, u32[]{:S(2)}) collective-permute-start(bf16[3,256]{1,0:T(4,128)(2,1)} %slice.312), channel_id=1, source_target_pairs={{0,4},{4,8},{8,12},{12,16},{16,20},{20,24},{24,28},{28,32},{32,36}... | collective-permute-start | bytes 4616 | tf_op jit(solution)/shard_map/ppermute | solution.py:24
  247.4 73.7 %collective-permute-start.6 = (bf16[4096,256]{1,0:T(8,128)(2,1)}, bf16[4096,256]{1,0:T(8,128)(2,1)}, u32[]{:S(2)}, u32[]{:S(2)}) collective-permute-start(bf16[4096,256]{1,0:T(8,128)(2,1)} %constant_dynamic-update-slice_fusion.5), channel_id=1, source_target_pairs={{0,128},{4,132},{8,136},{12,140},{16,144},{20,148},{24,152},{28,15... | collective-permute-start | bytes 6291464 | tf_op jit(solution)/shard_map/ppermute | solution.py:24
  495.8 33.8 %all-to-all-start.7 = ((f32[64,1,3072]{2,1,0:T(1,128)}), f32[64,1,3072]{2,1,0:T(1,128)S(1)}, u32[]{:S(2)}, u32[]{:S(2)}) async-start(f32[64,1,3072]{2,1,0:T(1,128)} %broadcast_in_dim.272), calls=%async_computation.7 | async-start | bytes 1572864 | tf_op jit(solution)/shard_map/all_to_all | solution.py:56
  (57 other events, 1719.6 us)
Sparse Core Ops, SparseCore 0:
  62.4 59.0 all-gather.11
  182.9 35.1 all-gather.7
  307.0 35.0 all-gather.9
where the time goes:
time: 542 us; the launch traced here: 538 us
  starting transfers between devices  198 us (37%)
  local copies, waits for them, and re-layouts  127 us (23%)
  loops' own time  46.8 us (9%)
  other arithmetic  41.6 us (8%)
  matrix products  36.6 us (7%)
  waiting for transfers between devices  35.3 us (7%)
  blocking collectives  33.2 us (6%)
  between operations  19.4 us (4%)
    ppermute x17, starting transfers between devices, shifted(): return lax.ppermute(block, axis, route)  125 us
    dynamic_slice x65, local copies, waits for them, and re-layouts, local(): lax.scan(sweep, initial, (stacked_keys, stacked_values, jnp.arange(block_...  47.6 us
    another operation x1, loops' own time, local(): lax.scan(sweep, initial, (stacked_keys, stacked_values, jnp.arange(block_...  44.5 us
    all_gather x3, blocking collectives, entering_2(): lax.all_gather(part.astype(kind), axis)  33.2 us
    unnamed x139, local copies, waits for them, and re-layouts  23.5 us
    slice x34, local copies, waits for them, and re-layouts, attend_piece(): query_pos[-1]  19.8 us
    dot_general x33, matrix products, compute(): jnp.einsum('gqts,sgd->gqtd', weights.astype(jnp.bfloat16), values_rank3,...  17.8 us
    all_to_all x1, starting transfers between devices, copy_for_each(): return lax.all_to_all(copies, axis, split_axis=0, concat_axis=0, tiled=True)  16.9 us
  transfers between devices with their start and end apart: 28, of which 8 were waited for; matrix products, arithmetic and copies ran while one was open for 36% of the time, Pallas kernels for 0%

commit v1 on v0

v1 whole, which is shorter than its diff:
```python
import math

import jax
import jax.numpy as jnp
from jax import lax
from jax.experimental import pallas as pl
from jax.experimental.pallas import tpu as pltpu
from jax.sharding import Mesh
from jax.sharding import PartitionSpec as P

AXES = ("X", "Y", "zl", "zh", "c")
MESH_ID = pl.DeviceIdType.MESH
BF = jnp.bfloat16
F32 = jnp.float32
HIGH = lax.Precision.HIGHEST
NEG_LARGE = -1e30
EPS_NORM = 1e-05
SUPER = 512
KV_ROWS = 5120
BACK = 4352
VM = pl.BlockSpec(memory_space=pltpu.VMEM)
SM = pl.BlockSpec(memory_space=pltpu.SMEM)
NT = (((1,), (1,)), ((), ()))
TN = (((0,), (0,)), ((), ()))


def coords():
    return tuple(lax.axis_index(a) for a in AXES)


def aligned(v, n):
    return pl.multiple_of(v, n)


def landed(dst, sem):
    pltpu.make_async_copy(dst, dst, sem).wait()


def exchange_in(
    q, k, v, x, b, c, dt,
    qo, kvo, xo, bo, co, dto, txo, tbo, tco,
    sq, rq, sx, rx, st, rt, sg, rg, sf, rf,
):
    X, Y, Z, H, C = coords()
    s = X * 4 + Y
    T = H * 2 + C
    u = Z * 4 + T
    zz = H * 4 + Z
    half = lax.div(Z, 2)
    bar = pltpu.get_barrier_semaphore()

    def signal(**where):
        pl.semaphore_signal(bar, 1, device_id=where, device_id_type=MESH_ID)

    def at(super_index):
        n = lax.rem(super_index + 16, 16)
        return {"X": lax.div(n, 4), "Y": lax.rem(n, 4)}

    def chip(o):
        n = lax.rem(zz + o, 8)
        return lax.div(n, 4), lax.rem(n, 4)

    others = [(o, e) for o in (1, 7, 2, 6, 3, 5, 4) for e in (0, 1)] + [(0, 1)]
    for o, e in others:
        zh, zl = chip(o)
        signal(zl=zl, zh=zh, c=lax.rem(C + e, 2))
    for d in range(1, 9):
        @pl.when(s >= d)
        def _():
            signal(**at(s - d))
    @pl.when(jnp.logical_and(C == 0, s >= 9))
    def _():
        signal(**at(s - 9), c=1)
    signal(**at(s - 1), zl=3, zh=1, c=1)

    kvo[0:128, :] = jnp.zeros((128, 256), BF)
    kvo[4864:5120, :] = jnp.zeros((256, 256), BF)

    expected = 15 + jnp.minimum(8, 15 - s)
    expected += jnp.where(jnp.logical_and(C == 1, s <= 6), 1, 0)
    expected += jnp.where(u == 15, 16, 0)
    pl.semaphore_wait(bar, expected)

    srow = lax.rem(Z, 2) * 128 + T * 32
    slot = lax.rem(Z, 2) * 4 + T

    def qkv_parts(o):
        zh, zl = chip(o)
        g = zh * 4 + zl
        krow = BACK + half * 256 + srow
        k_dst = kvo.at[pl.ds(aligned(krow, 32), 32), 0:128]
        v_dst = kvo.at[pl.ds(aligned(krow, 32), 32), 128:256]
        q_dst = qo.at[pl.ds(aligned(srow, 32), 32), :]
        k_src = k.at[:, pl.ds(aligned(g * 128, 128), 128)]
        v_src = v.at[:, pl.ds(aligned(g * 128, 128), 128)]
        q_src = q.at[:, pl.ds(aligned(g * 512, 512), 512)]
        return {"zh": zh, "zl": zl, "c": half}, ((k_src, k_dst), (v_src, v_dst), (q_src, q_dst))

    def qkv_copy(o, i):
        where, parts = qkv_parts(o)
        src, dst = parts[i]
        return pltpu.make_async_remote_copy(
            src, dst, sq.at[i, o], rq.at[i, slot], device_id=where, device_id_type=MESH_ID
        )

    order8 = (4, 3, 5, 2, 6, 1, 7)
    for o in order8:
        qkv_copy(o, 0).start()
        qkv_copy(o, 1).start()

    @pl.when(half != C)
    def _():
        qkv_copy(0, 0).start()
        qkv_copy(0, 1).start()

    @pl.when(half == C)
    def _():
        for src, dst in qkv_parts(0)[1]:
            dst[...] = src[...]

    def col_parts(o, e):
        zh, zl = chip(o)
        cc = lax.rem(C + e, 2)
        tensor = zh * 2 + cc
        xcol = tensor * 2048 + zl * 512
        gcol = (tensor * 2 + lax.div(zl, 2)) * 128
        rows = pl.ds(aligned(u * 32, 32), 32)
        wide = pl.ds(aligned(xcol, 512), 512)
        thin = pl.ds(aligned(gcol, 128), 128)
        return {"zh": zh, "zl": zl, "c": cc}, (
            (dt, dto.at[rows, :]),
            (b.at[:, thin], bo.at[rows, :]),
            (c.at[:, thin], co.at[rows, :]),
            (x.at[:, wide], xo.at[rows, :]),
        )

    def col_copy(o, e, i):
        where, parts = col_parts(o, e)
        src, dst = parts[i]
        return pltpu.make_async_remote_copy(
            src, dst, sx.at[i, o * 2 + e], rx.at[i, u], device_id=where, device_id_type=MESH_ID
        )

    order16 = [(o, e) for o in order8 for e in (0, 1)] + [(0, 1)]
    for i in range(3):
        for o, e in order16:
            col_copy(o, e, i).start()

    def tail_copy(o, e, i):
        zh, zl = chip(o)
        cc = lax.rem(C + e, 2)
        tensor = zh * 2 + cc
        xcol = tensor * 2048 + zl * 512
        gcol = (tensor * 2 + lax.div(zl, 2)) * 128
        src, dst, col, wide = ((x, txo, xcol, 512), (b, tbo, gcol, 128), (c, tco, gcol, 128))[i]
        return pltpu.make_async_remote_copy(
            src.at[16:32, pl.ds(aligned(col, wide), wide)], dst,
            st.at[i, o * 2 + e], rt.at[i],
            device_id={**at(s + 1), "zh": zh, "zl": zl, "c": cc}, device_id_type=MESH_ID,
        )

    for o, e in order16:
        col_copy(o, e, 3).start()
    for i, (src, dst) in enumerate(col_parts(0, 0)[1]):
        dst[...] = src[...]

    @pl.when(u == 15)
    def _():
        for o in range(8):
            for e in (0, 1):
                for i in range(3):
                    tail_copy(o, e, i).start()

    for o in order8:
        qkv_copy(o, 2).start()

    @pl.when(half != C)
    def _():
        qkv_copy(0, 2).start()

    def qkv_landed(i):
        for j in range(2):
            for t in range(4):
                row = j * 128 + t * 32
                if i == 2:
                    dst = qo.at[row:row + 32, :]
                else:
                    krow = aligned(BACK + C * 256 + row, 32)
                    dst = kvo.at[pl.ds(krow, 32), i * 128:i * 128 + 128]

                @pl.when(jnp.logical_or(2 * C + j != Z, T != t))
                def _():
                    landed(dst, rq.at[i, j * 4 + t])

    qkv_landed(0)
    qkv_landed(1)

    def half_rows(d):
        return kvo.at[pl.ds(aligned(BACK - SUPER * d + C * 256, 256), 256), :]

    def partner_rows(d):
        return kvo.at[pl.ds(aligned(BACK - SUPER * d + (1 - C) * 256, 256), 256), :]

    def pass_on(d):
        return pltpu.make_async_remote_copy(
            half_rows(0), half_rows(d), sg.at[d], rg.at[d], device_id=at(s + d), device_id_type=MESH_ID
        )

    def pass_last():
        return pltpu.make_async_remote_copy(
            kvo.at[BACK + 384:BACK + 512, :], kvo.at[128:256, :], sg.at[9], rg.at[9],
            device_id={**at(s + 9), "c": 0}, device_id_type=MESH_ID,
        )

    def to_partner(d):
        return pltpu.make_async_remote_copy(
            half_rows(d), half_rows(d), sf.at[d], rf.at[d], device_id={"c": 1 - C}, device_id_type=MESH_ID
        )

    last_out = jnp.logical_and(C == 1, s <= 6)
    for d in range(1, 9):
        @pl.when(s + d < 16)
        def _():
            pass_on(d).start()

    @pl.when(last_out)
    def _():
        pass_last().start()

    to_partner(0).start()
    for d in range(1, 9):
        @pl.when(s >= d)
        def _():
            landed(half_rows(d), rg.at[d])
            to_partner(d).start()

    for i in range(4):
        for o, e in order16:
            zs = lax.rem(zz + 8 - o, 8)
            us = lax.rem(zs, 4) * 4 + lax.div(zs, 4) * 2 + lax.rem(C + e, 2)
            dst = (dto, bo, co, xo)[i].at[pl.ds(aligned(us * 32, 32), 32), :]
            landed(dst, rx.at[i, us])
    for i in range(3):
        landed((txo, tbo, tco)[i], rt.at[i])
    qkv_landed(2)

    @pl.when(jnp.logical_and(C == 0, s >= 9))
    def _():
        landed(kvo.at[128:256, :], rg.at[9])

    landed(partner_rows(0), rf.at[0])
    for d in range(1, 9):
        @pl.when(s >= d)
        def _():
            landed(partner_rows(d), rf.at[d])

    for i in range(3):
        for o in order8:
            qkv_copy(o, i).wait_send()

        @pl.when(half != C)
        def _():
            qkv_copy(0, i).wait_send()
    for i in range(4):
        for o, e in order16:
            col_copy(o, e, i).wait_send()

    @pl.when(u == 15)
    def _():
        for o in range(8):
            for e in (0, 1):
                for i in range(3):
                    tail_copy(o, e, i).wait_send()
    to_partner(0).wait_send()
    for d in range(1, 9):
        @pl.when(s + d < 16)
        def _():
            pass_on(d).wait_send()

        @pl.when(s >= d)
        def _():
            to_partner(d).wait_send()

    @pl.when(last_out)
    def _():
        pass_last().wait_send()


def call_exchange_in(arrays):
    shapes = ((256, 512), (KV_ROWS, 256), (512, 512), (512, 128), (512, 128), (512, 128),
              (16, 512), (16, 128), (16, 128))
    dma = pltpu.SemaphoreType.DMA
    return pl.pallas_call(
        exchange_in,
        out_shape=[jax.ShapeDtypeStruct(n, BF) for n in shapes],
        in_specs=[VM] * 7,
        out_specs=[VM] * 9,
        scratch_shapes=[
            dma((3, 8)), dma((3, 8)), dma((4, 16)), dma((4, 16)), dma((3, 16)), dma((3,)),
            dma((10,)), dma((10,)), dma((9,)), dma((9,)),
        ],
        compiler_params=pltpu.CompilerParams(collective_id=1, has_side_effects=True),
        name="exchange_in",
    )(*arrays)


def spread_matrix(rows, cols):
    a = lax.broadcasted_iota(jnp.int32, (rows, cols), 0)
    b = lax.broadcasted_iota(jnp.int32, (rows, cols), 1)
    if rows < cols:
        return (lax.div(b, 64) == a).astype(F32)
    return (lax.div(a, 64) == b).astype(F32)


def dot(a, b, dims=(((1,), (0,)), ((), ())), precision=None):
    return lax.dot_general(a, b, dims, precision=precision, preferred_element_type=F32)


def doc_of(pos, s1, s2):
    one = jnp.where(pos >= s1, 1, 0) + jnp.where(pos >= s2, 1, 0)
    return jnp.where(pos >= 0, one, -1)


def softplus(z):
    return jnp.maximum(z, 0.0) + jnp.log1p(jnp.exp(-jnp.abs(z)))


def mamba_local(
    lens, x, b, c, dt, tx, tb, tc, conv_x, conv_b, conv_c, bias, rate, skip,
    base_o, inflow_o, cc_o, part_o, decay_o, send_o,
    xs, bs, cs,
):
    X, Y, Z, H, C = coords()
    s = X * 4 + Y
    T = H * 2 + C
    s1 = lens[0]
    s2 = lens[0] + lens[1]
    p0 = s * SUPER
    lane8 = lax.broadcasted_iota(jnp.int32, (8, 32), 1)
    sub8 = lax.broadcasted_iota(jnp.int32, (8, 32), 0)
    own = lane8 == sub8 + 8 * Z

    def column(ref):
        return jnp.sum(jnp.where(own, ref[...], 0.0), axis=1, keepdims=True)

    pick32 = (lax.broadcasted_iota(jnp.int32, (32, 8), 0)
              == lax.broadcasted_iota(jnp.int32, (32, 8), 1) + 8 * Z).astype(F32)

    def row(ref):
        return dot(ref[...], pick32, precision=HIGH)

    first_head = T * 32 + Z * 8
    pick = (lax.broadcasted_iota(jnp.int32, (128, 8), 0)
            == lax.broadcasted_iota(jnp.int32, (128, 8), 1) + first_head).astype(BF)
    dcol = softplus(dot(dt[...], pick) + row(bias))
    drow = softplus(dot(pick, dt[...], (((0,), (1,)), ((), ()))) + column(bias))
    lcol = -dcol * row(rate)
    lrow = -drow * column(rate)
    wide = spread_matrix(8, 512)
    tall = spread_matrix(512, 8)
    skip_wide = dot(row(skip), wide, precision=HIGH)

    for src, tail, buf in ((x, tx, xs), (b, tb, bs), (c, tc, cs)):
        buf[0:16, :] = tail[...].astype(F32)
        buf[16:528, :] = src[...].astype(F32)
    taps_x = conv_x[:, pl.ds(aligned(Z * 512, 512), 512)].astype(F32)
    group = pl.ds(aligned(lax.div(Z, 2) * 128, 128), 128)
    taps_b = conv_b[:, group].astype(F32)
    taps_c = conv_c[:, group].astype(F32)

    ti = lax.broadcasted_iota(jnp.int32, (128, 128), 0)
    si = lax.broadcasted_iota(jnp.int32, (128, 128), 1)
    lower = (ti >= si).astype(F32)
    upper = (ti <= si).astype(F32)
    lane = lax.broadcasted_iota(jnp.int32, (128, 128), 1)
    state = jnp.zeros((512, 128), F32)
    decay = jnp.ones((8, 128), F32)
    for n in range(4):
        pb = p0 + n * 128
        rows = slice(n * 128, n * 128 + 128)
        pcol = pb + lax.broadcasted_iota(jnp.int32, (128, 1), 0)
        prow = pb + lax.broadcasted_iota(jnp.int32, (1, 128), 1)
        start = jnp.where(pcol >= s2, s2, jnp.where(pcol >= s1, s1, 0))
        keep = [pcol - j >= start for j in range(4)]

        def conv(buf, taps):
            total = None
            for j in range(4):
                lo = 16 + n * 128 - j
                term = taps[j:j + 1, :] * buf[lo:lo + 128, :]
                if j:
                    term = jnp.where(keep[j], term, 0.0)
                total = term if total is None else total + term
            return (total / (1.0 + jnp.exp(-total))).astype(BF)

        xc = conv(xs, taps_x)
        bc = conv(bs, taps_b)
        cc = conv(cs, taps_c)
        cc_o[rows, :] = cc
        ccol = dot(lower, lcol[rows, :], precision=HIGH)
        crow = dot(lrow[:, rows], upper, precision=HIGH)
        dcol_n = dcol[rows, :]
        drow_n = drow[:, rows]
        doc_c = doc_of(pcol, s1, s2)
        doc_r = doc_of(prow, s1, s2)
        allowed = jnp.logical_and(ti >= si, doc_c == doc_r)
        cross = jnp.where(allowed, dot(cc, bc, NT), 0.0)
        xf = xc.astype(F32)
        for pair in range(4):
            mixes = []
            for h in (2 * pair, 2 * pair + 1):
                gap = ccol[:, h:h + 1] - crow[h:h + 1, :]
                seg = jnp.exp(jnp.minimum(gap, 0.0))
                mixes.append((seg * cross * drow_n[h:h + 1, :]).astype(BF))
            xp = xc[:, pair * 128:pair * 128 + 128]
            zero = jnp.zeros_like(xp)
            both = jnp.concatenate(
                [jnp.where(lane < 64, xp, zero), jnp.where(lane < 64, zero, xp)], axis=0)
            intra = dot(jnp.concatenate(mixes, axis=1), both)
            cols = slice(pair * 128, pair * 128 + 128)
            base_o[rows, cols] = intra + skip_wide[:, cols] * xf[:, cols]
        pe = pb + 127
        doc_e = doc_of(pe, s1, s2)
        doc_p = doc_of(pb - 1, s1, s2)
        to_end = jnp.where(doc_c == doc_e, jnp.exp(ccol[127:128, :] - ccol), 0.0) * dcol_n
        weighted = (dot(to_end, wide, precision=HIGH) * xf).astype(BF)
        local = dot(weighted, bc, TN)
        factor = jnp.where(doc_p == doc_e, jnp.exp(crow[:, 127:128]), 0.0)
        factor = jnp.broadcast_to(factor, (8, 128))
        inflow_o[rows, :] = jnp.where(doc_c == doc_p, jnp.exp(ccol), 0.0)
        state = dot(tall, factor, precision=HIGH) * state + local
        decay = factor * decay
        if n < 3:
            part_o[n] = state
            decay_o[n] = decay
    for j in range(16):
        send_o[j, 0:32, :] = state[j * 32:j * 32 + 32, :]
        send_o[j, 32:40, :] = jnp.broadcast_to(decay[j // 2:j // 2 + 1, :], (8, 128))


def call_mamba_local(*args):
    out = [((512, 512), F32), ((512, 8), F32), ((512, 128), BF), ((3, 512, 128), F32),
           ((3, 8, 128), F32), ((16, 40, 128), F32)]
    return pl.pallas_call(
        mamba_local,
        out_shape=[jax.ShapeDtypeStruct(n, t) for n, t in out],
        in_specs=[SM] + [VM] * 13,
        out_specs=[VM] * 6,
        scratch_shapes=[pltpu.VMEM((528, 512), F32), pltpu.VMEM((528, 128), F32),
                        pltpu.VMEM((528, 128), F32)],
        name="mamba_local",
    )(*args)


def pass_states(send, inc, got, back, s1, r1, s2, r2):
    X, Y, Z, H, C = coords()
    s = X * 4 + Y
    bar = pltpu.get_barrier_semaphore()

    def peer(d):
        n = lax.rem(s + d, 16)
        return n, {"X": lax.div(n, 4), "Y": lax.rem(n, 4)}

    for d in range(1, 16):
        pl.semaphore_signal(bar, 1, device_id=peer(d)[1], device_id_type=MESH_ID)
    pl.semaphore_wait(bar, 15)

    def there(d):
        n, where = peer(d)
        return pltpu.make_async_remote_copy(
            send.at[n], got.at[s], s1.at[d], r1.at[s], device_id=where, device_id_type=MESH_ID)

    def again(d):
        n, where = peer(d)
        rows = pl.ds(aligned(s * 32, 32), 32)
        return pltpu.make_async_remote_copy(
            back.at[n], inc.at[rows, :], s2.at[d], r2.at[s], device_id=where, device_id_type=MESH_ID)

    for d in range(1, 16):
        there(d).start()
    got[s] = send[s]
    for d in range(1, 16):
        n, _ = peer(16 - d)
        landed(got.at[n], r1.at[n])
    value = jnp.zeros((4, 8, 128), F32)
    for n in range(16):
        back[n] = value.reshape(32, 128).astype(BF)
        value = got[n, 32:40, :][None] * value + got[n, 0:32, :].reshape(4, 8, 128)
    for d in range(1, 16):
        again(d).start()
    inc[pl.ds(aligned(s * 32, 32), 32), :] = back[s]
    for d in range(1, 16):
        n, _ = peer(16 - d)
        landed(inc.at[pl.ds(aligned(n * 32, 32), 32), :], r2.at[n])
    for d in range(1, 16):
        there(d).wait_send()
        again(d).wait_send()


def call_pass_states(send):
    dma = pltpu.SemaphoreType.DMA
    return pl.pallas_call(
        pass_states,
        out_shape=jax.ShapeDtypeStruct((512, 128), BF),
        in_specs=[VM],
        out_specs=VM,
        scratch_shapes=[pltpu.VMEM((16, 40, 128), F32), pltpu.VMEM((16, 32, 128), BF),
                        dma((16,)), dma((16,)), dma((16,)), dma((16,))],
        compiler_params=pltpu.CompilerParams(collective_id=2, has_side_effects=True),
        name="pass_states",
    )(send)


def mamba_finish(base, inflow, cc, part, decay, inc, gain, out, sums):
    Z = lax.axis_index("zl")
    wide = spread_matrix(8, 512)
    tall = spread_matrix(512, 8)
    gain_row = gain[:, pl.ds(aligned(Z * 512, 512), 512)]
    a = lax.broadcasted_iota(jnp.int32, (128, 128), 0)
    b = lax.broadcasted_iota(jnp.int32, (128, 128), 1)
    average = jnp.where(lax.div(a, 64) == lax.div(b, 64), 1.0 / 64, 0.0).astype(F32)
    entering = inc[...].astype(F32)
    total = jnp.zeros((1, 512), F32)
    for n in range(4):
        rows = slice(n * 128, n * 128 + 128)
        if n == 0:
            state = inc[...]
        else:
            state = (dot(tall, decay[n - 1], precision=HIGH) * entering + part[n - 1]).astype(BF)
        flow = dot(inflow[rows, :], wide, precision=HIGH)
        full = base[rows, :] + dot(cc[rows, :], state, NT) * flow
        for pair in range(4):
            cols = slice(pair * 128, pair * 128 + 128)
            f = full[:, cols]
            mean = dot(f * f, average, precision=HIGH)
            out[rows, cols] = (f * lax.rsqrt(mean + EPS_NORM) * gain_row[:, cols]).astype(BF)
        total = total + jnp.sum(out[rows, :].astype(F32), axis=0, keepdims=True)
    for i in range(4):
        sums[i:i + 1, :] = total[:, i * 128:i * 128 + 128]
    sums[4:8, :] = jnp.zeros((4, 128), F32)


def call_mamba_finish(*args):
    return pl.pallas_call(
        mamba_finish,
        out_shape=[jax.ShapeDtypeStruct((512, 512), BF), jax.ShapeDtypeStruct((8, 128), F32)],
        in_specs=[VM] * 7,
        out_specs=[VM] * 2,
        name="mamba_finish",
    )(*args)


def attend(windows, lens, q, kv, msum, out, sums, scores, top, acc, tot):
    X, Y, Z, H, C = coords()
    s = X * 4 + Y
    t0 = s * SUPER + C * 256
    base = s * SUPER - BACK
    s1 = lens[0]
    s2 = lens[0] + lens[1]
    scale = math.log2(math.e) / math.sqrt(128)

    def doc_start(t):
        return jnp.where(t >= s2, s2, jnp.where(t >= s1, s1, 0))

    tcol = t0 + lax.broadcasted_iota(jnp.int32, (256, 1), 0)
    start_col = doc_start(tcol)
    lane = lax.broadcasted_iota(jnp.int32, (1, 512), 1)
    end_row = BACK + C * 256 + 256
    sums[0:4, :] = msum[0:4, :]
    for h in range(4):
        w = windows[(H * 4 + Z) * 4 + h]
        low = jnp.maximum(tcol - w + 1, start_col)
        low_first = jnp.maximum(t0 - w + 1, doc_start(t0))
        c0 = lax.div(low_first - base, 256)
        count = lax.div(end_row - c0 * 256 + 511, 512)
        qh = q[:, h * 128:h * 128 + 128]
        top[...] = jnp.full((256, 128), NEG_LARGE, F32)
        acc[...] = jnp.zeros((256, 128), F32)
        tot[...] = jnp.zeros((256, 128), F32)

        @pl.loop(0, count)
        def _(i):
            r = aligned(c0 * 256 + i * 512, 256)
            score = dot(qh, kv[pl.ds(r, 512), 0:128], NT)
            kpos = base + r + lane
            ok = jnp.logical_and(kpos >= low, kpos <= tcol)
            score = jnp.where(ok, score, NEG_LARGE)
            scores[:, pl.ds(aligned(i * 512, 512), 512)] = score
            best = jnp.maximum(jnp.maximum(score[:, 0:128], score[:, 128:256]),
                               jnp.maximum(score[:, 256:384], score[:, 384:512]))
            top[...] = jnp.maximum(top[...], best)

        best = jnp.max(top[...], axis=1, keepdims=True)

        @pl.loop(0, count)
        def _(i):
            r = aligned(c0 * 256 + i * 512, 256)
            weight = jnp.exp2((scores[:, pl.ds(aligned(i * 512, 512), 512)] - best) * scale)
            tot[...] += ((weight[:, 0:128] + weight[:, 128:256])
                         + (weight[:, 256:384] + weight[:, 384:512]))
            acc[...] += dot(weight.astype(BF), kv[pl.ds(r, 512), 128:256])

        total = jnp.sum(tot[...], axis=1, keepdims=True)
        result = (acc[...] / total).astype(BF)
        out[:, h * 128:h * 128 + 128] = result
        sums[4 + h:5 + h, :] = jnp.sum(result.astype(F32), axis=0, keepdims=True)


def call_attend(*args):
    return pl.pallas_call(
        attend,
        out_shape=[jax.ShapeDtypeStruct((256, 512), BF), jax.ShapeDtypeStruct((8, 128), F32)],
        in_specs=[SM, SM, VM, VM, VM],
        out_specs=[VM] * 2,
        scratch_shapes=[pltpu.VMEM((256, 4608), F32), pltpu.VMEM((256, 128), F32),
                        pltpu.VMEM((256, 128), F32), pltpu.VMEM((256, 128), F32)],
        name="attend",
    )(*args)


def exchange_out(
    att, mam, sums, ao, mo, asum, msum,
    buf_y, buf_x, buf_f, send_x, send_f, sa, ra, sm, rm, sc, ry, rx, rf,
):
    X, Y, Z, H, C = coords()
    half = lax.div(Z, 2)
    bar = pltpu.get_barrier_semaphore()
    near = [(o, e) for o in range(4) for e in (0, 1) if o or e]

    def near_id(o, e):
        return {"zl": lax.rem(Z + o, 4), "c": lax.rem(C + e, 2)}

    for o, e in near:
        pl.semaphore_signal(bar, 1, device_id=near_id(o, e), device_id_type=MESH_ID)
    for d in range(1, 4):
        for name, mine in (("X", X), ("Y", Y)):
            pl.semaphore_signal(
                bar, 1, device_id={name: lax.rem(mine + d, 4)}, device_id_type=MESH_ID)
    pl.semaphore_wait(bar, 13)

    def along(name, mine, d, src, buf, recv, first):
        return pltpu.make_async_remote_copy(
            src, buf.at[mine], sc.at[first + d], recv.at[mine],
            device_id={name: lax.rem(mine + d, 4)}, device_id_type=MESH_ID)

    def cols_of(block):
        return pl.ds(aligned(block * 512, 512), 512)

    def mam_copy(o):
        zl = lax.rem(Z + o, 4)
        return pltpu.make_async_remote_copy(
            mam.at[pl.ds(aligned(zl * 128, 128), 128), :], mo.at[:, cols_of(Z)],
            sm.at[o], rm.at[Z], device_id={"zl": zl}, device_id_type=MESH_ID)

    def att_copy(j):
        return pltpu.make_async_remote_copy(
            att.at[j * 128:j * 128 + 128, :], ao.at[:, cols_of(lax.rem(Z, 2))],
            sa.at[j], ra.at[lax.rem(Z, 2)],
            device_id={"zl": 2 * C + j, "c": half}, device_id_type=MESH_ID)

    for d in range(1, 4):
        along("Y", Y, d, sums, buf_y, ry, 0).start()
    for o in (2, 1, 3):
        mam_copy(o).start()
    for j in range(2):
        mine = jnp.logical_and(2 * C + j == Z, half == C)

        @pl.when(jnp.logical_not(mine))
        def _():
            att_copy(j).start()

        @pl.when(mine)
        def _():
            ao[:, cols_of(lax.rem(Z, 2))] = att[j * 128:j * 128 + 128, :]
    buf_y[Y] = sums[...]
    mo[:, cols_of(Z)] = mam[pl.ds(aligned(Z * 128, 128), 128), :]

    for d in range(1, 4):
        n = lax.rem(Y + d, 4)
        landed(buf_y.at[n], ry.at[n])
    send_x[...] = (buf_y[0] + buf_y[1]) + (buf_y[2] + buf_y[3])
    for d in range(1, 4):
        along("X", X, d, send_x, buf_x, rx, 4).start()
    buf_x[X] = send_x[...]
    for d in range(1, 4):
        n = lax.rem(X + d, 4)
        landed(buf_x.at[n], rx.at[n])
    send_f[...] = (buf_x[0] + buf_x[1]) + (buf_x[2] + buf_x[3])
    place = Z * 2 + C

    def last_copy(o, e):
        return pltpu.make_async_remote_copy(
            send_f, buf_f.at[place], sc.at[8 + o * 2 + e], rf.at[place],
            device_id=near_id(o, e), device_id_type=MESH_ID)

    for o, e in near:
        last_copy(o, e).start()
    buf_f[place] = send_f[...]
    for o, e in near:
        n = lax.rem(Z + o, 4) * 2 + lax.rem(C + e, 2)
        landed(buf_f.at[n], rf.at[n])
    for n in range(4):
        msum[n * 4:n * 4 + 4, :] = buf_f[n * 2 + C, 0:4, :]
    for j in range(2):
        first = (2 * C + j) * 2
        asum[j * 4:j * 4 + 4, :] = buf_f[first, 4:8, :] + buf_f[first + 1, 4:8, :]

    for o in range(1, 4):
        n = lax.rem(Z + o, 4)
        landed(mo.at[:, cols_of(n)], rm.at[n])
    for j in range(2):
        @pl.when(jnp.logical_or(2 * C + j != Z, half != C))
        def _():
            landed(ao.at[:, j * 512:j * 512 + 512], ra.at[j])

    for d in range(1, 4):
        along("Y", Y, d, sums, buf_y, ry, 0).wait_send()
        along("X", X, d, send_x, buf_x, rx, 4).wait_send()
        mam_copy(d).wait_send()
    for o, e in near:
        last_copy(o, e).wait_send()
    for j in range(2):
        @pl.when(jnp.logical_or(2 * C + j != Z, half != C))
        def _():
            att_copy(j).wait_send()


def call_exchange_out(*args):
    dma = pltpu.SemaphoreType.DMA
    tile = pltpu.VMEM((8, 128), F32)
    return pl.pallas_call(
        exchange_out,
        out_shape=[jax.ShapeDtypeStruct((128, 1024), BF), jax.ShapeDtypeStruct((128, 2048), BF),
                   jax.ShapeDtypeStruct((8, 128), F32), jax.ShapeDtypeStruct((16, 128), F32)],
        in_specs=[VM] * 3,
        out_specs=[VM] * 4,
        scratch_shapes=[
            pltpu.VMEM((4, 8, 128), F32), pltpu.VMEM((4, 8, 128), F32), pltpu.VMEM((8, 8, 128), F32),
            tile, tile, dma((2,)), dma((2,)), dma((4,)), dma((4,)), dma((16,)),
            dma((4,)), dma((4,)), dma((8,)),
        ],
        compiler_params=pltpu.CompilerParams(collective_id=3, has_side_effects=True),
        name="exchange_out",
    )(*args)


def local(
    queries, keys, values, mamba_x, mamba_b, mamba_c, mamba_dt, conv_x, conv_b, conv_c,
    dt_bias, decay_rate, skip_gain, norm_gain, windows, doc_lengths,
):
    q, kv, x, b, c, dt, tx, tb, tc = call_exchange_in(
        (queries, keys, values, mamba_x, mamba_b, mamba_c, mamba_dt))
    base, inflow, cc, part, decay, send = call_mamba_local(
        doc_lengths, x, b, c, dt, tx, tb, tc, conv_x, conv_b, conv_c,
        dt_bias.reshape(1, 32), decay_rate.reshape(1, 32), skip_gain.reshape(1, 32))
    inc = call_pass_states(send)
    mam, msum = call_mamba_finish(
        base, inflow, cc, part, decay, inc, norm_gain.reshape(1, 2048))
    att, sums = call_attend(windows, doc_lengths, q, kv, msum)
    ao, mo, asum, ms = call_exchange_out(att, mam, sums)
    return ao, mo, asum.reshape(1024), ms.reshape(2048)


def solution(mesh):
    torus = Mesh(mesh.devices.reshape(4, 4, 4, 2, 2), AXES)
    tokens = P(AXES, None)
    tensor = ("zh", "c")
    in_specs = (tokens,) * 7 + (P(None, tensor),) * 3 + (P(tensor),) * 4 + (P(), P())
    out_specs = (P(("X", "Y", "zl"), tensor), P(("X", "Y", "zl"), tensor), P(tensor), P(tensor))
    return jax.shard_map(local, mesh=torus, in_specs=in_specs, out_specs=out_specs, check_vma=False)
```

time: 542 us -> 127 us (0.23)
  the two profiles are of different devices: /device:TPU:128 before, /device:TPU:1 now
where the time goes in v1:
time: 127 us; the launch traced here: 125 us
  Pallas kernels  118 us (93%)
  local copies, waits for them, and re-layouts  6.12 us (5%)
    pallas_call x1, Pallas kernels, call_exchange_in(): pl.pallas_call(exchange_in, out_shape=[jax.ShapeDtypeStruct(n, BF) for n...  47.3 us
    pallas_call x1, Pallas kernels, call_exchange_out(): pl.pallas_call(exchange_out, out_shape=[jax.ShapeDtypeStruct((128, 1024),...  32.4 us
    pallas_call x1, Pallas kernels, call_pass_states(): pl.pallas_call(pass_states, out_shape=jax.ShapeDtypeStruct((512, 128), BF...  20 us
    pallas_call x1, Pallas kernels, call_mamba_local(): pl.pallas_call(mamba_local, out_shape=[jax.ShapeDtypeStruct(n, t) for n,...  7.56 us
    unnamed x4, local copies, waits for them, and re-layouts  6.12 us
    pallas_call x1, Pallas kernels, call_mamba_finish(): pl.pallas_call(mamba_finish, out_shape=[jax.ShapeDtypeStruct((512, 512),...  5.72 us
    pallas_call x1, Pallas kernels, call_attend(): pl.pallas_call(attend, out_shape=[jax.ShapeDtypeStruct((256, 512), BF), j...  5.36 us

profile of v1, /device:TPU:1, one launch (start us, length us, event | category | flops | bytes accessed | tf_op | source)
XLA Modules:
  0.0 125.1 jit_solution(3327846208588140592)
XLA Ops:
  0.6 47.3 %exchange_in.1 = (bf16[256,512]{1,0:T(8,128)(2,1)}, bf16[5120,256]{1,0:T(8,128)(2,1)}, bf16[512,512]{1,0:T(8,128)(2,1)}, bf16[512,128]{1,0:T(8,128)(2,1)}, bf16[...) custom-call(bf16[32,4096]{1,0:T(8,128)(2,1)} %q.1, ...), custom_call_target="tpu_custom_call" | custom-call | tf_op jit(solution)/shard_map/exchange_in/pallas_call | solution.py:293
  47.9 7.6 %mamba_local.1 = (f32[512,512]{1,0:T(8,128)}, f32[512,8]{1,0:T(8,128)}, bf16[512,128]{1,0:T(8,128)(2,1)}, f32[3,512,128]{2,1,0:T(8,128)}, f32[3,8,128]{2,1,0:T(8,128)}, /*index=5*/f32[16,40,128]{2,1,0:T(8,128)}) custom-call(s32[3]{0:T(128)} %lens.3, bf16[512,512]{1,0:T(8,128)(2,1)} %get-tuple-element.29.x, bf16[512,128]{1,0:T(8,128)(2,1)} %get-tuple-element.30.b, ...), custom_call_target="tpu_custom_call" | custom-call | tf_op jit(solution)/shard_map/mamba_local/pallas_call | solution.py:444
  55.5 20.0 %pass_states.1.inc = bf16[512,128]{1,0:T(8,128)(2,1)} custom-call(f32[16,40,128]{2,1,0:T(8,128)} %get-tuple-element.41.send), custom_call_target="tpu_custom_call" | custom-call | tf_op jit(solution)/shard_map/pass_states/pallas_call | solution.py:502
  75.5 5.7 %mamba_finish.1 = (bf16[512,512]{1,0:T(8,128)(2,1)}, f32[8,128]{1,0:T(8,128)}) custom-call(f32[512,512]{1,0:T(8,128)} %get-tuple-element.36.base, f32[512,8]{1,0:T(8,128)} %get-tuple-element.37.inflow, bf16[512,128]{1,0:T(8,128)(2,1)} %get-tuple-element.38.cc, f32[3,512,128]{2,1,0:T(8,128)} %get-tuple-element.39.part, f32[3,8,128]{2,1,0:T(8,128)} %get-tuple-element.40.decay, ...), custom_call_target="tpu_custom_call" | custom-call | tf_op jit(solution)/shard_map/mamba_finish/pallas_call | solution.py:544
  81.2 5.4 %attend.1 = (bf16[256,512]{1,0:T(8,128)(2,1)}, f32[8,128]{1,0:T(8,128)}) custom-call(s32[32]{0:T(128)} %windows.1, s32[3]{0:T(128)} %lens.3, bf16[256,512]{1,0:T(8,128)(2,1)} %get-tuple-element.27.q, bf16[5120,256]{1,0:T(8,128)(2,1)} %get-tuple-element.28.kv, f32[8,128]{1,0:T(8,128)} %get-tuple-element.42.msum), custom_call_target="tpu_custom_call" | custom-call | tf_op jit(solution)/shard_map/attend/pallas_call | solution.py:610
  86.6 32.4 %exchange_out.1 = (bf16[128,1024]{1,0:T(8,128)(2,1)}, bf16[128,2048]{1,0:T(8,128)(2,1)}, f32[8,128]{1,0:T(8,128)}, f32[16,128]{1,0:T(8,128)}) custom-call(bf16[256,512]{1,0:T(8,128)(2,1)} %get-tuple-element.43.att, bf16[512,512]{1,0:T(8,128)(2,1)} %get-tuple-element.44.mam, f32[8,128]{1,0:T(8,128)} %get-tuple-element.45.sums), custom_call_target="tpu_custom_call" | custom-call | tf_op jit(solution)/shard_map/exchange_out/pallas_call | solution.py:731
  119.0 1.7 %copy.24 = bf16[128,1024]{1,0:T(8,128)(2,1)} copy(bf16[128,1024]{1,0:T(8,128)(2,1)} %get-tuple-element.54) | data formatting | bytes 524288
  120.7 1.9 %copy.25 = bf16[128,2048]{1,0:T(8,128)(2,1)} copy(bf16[128,2048]{1,0:T(8,128)(2,1)} %get-tuple-element.55) | data formatting | bytes 1048576
  122.6 1.3 %copy.26 = f32[1024]{0:T(1024)} copy(f32[1024]{0:T(1024)} %bitcast.8) | data formatting | bytes 8192
  123.8 1.3 %copy.27 = f32[2048]{0:T(1024)} copy(f32[2048]{0:T(1024)} %bitcast.7) | data formatting | bytes 16384

commit v2 on v1

v2 whole, which is shorter than its diff:
```python
import math

import jax
import jax.numpy as jnp
from jax import lax
from jax.experimental import pallas as pl
from jax.experimental.pallas import tpu as pltpu
from jax.sharding import Mesh
from jax.sharding import PartitionSpec as P

AXES = ("X", "Y", "zl", "zh", "c")
MESH_ID = pl.DeviceIdType.MESH
BF = jnp.bfloat16
F32 = jnp.float32
HIGH = lax.Precision.HIGHEST
NEG_LARGE = -1e30
EPS_NORM = 1e-05
SUPER = 512
KV_ROWS = 5120
BACK = 4352
VM = pl.BlockSpec(memory_space=pltpu.VMEM)
SM = pl.BlockSpec(memory_space=pltpu.SMEM)
NT = (((1,), (1,)), ((), ()))
TN = (((0,), (0,)), ((), ()))


def coords():
    return tuple(lax.axis_index(a) for a in AXES)


def aligned(v, n):
    return pl.multiple_of(v, n)


def landed(dst, sem):
    pltpu.make_async_copy(dst, dst, sem).wait()


def spread_matrix(rows, cols):
    a = lax.broadcasted_iota(jnp.int32, (rows, cols), 0)
    b = lax.broadcasted_iota(jnp.int32, (rows, cols), 1)
    if rows < cols:
        return (lax.div(b, 64) == a).astype(F32)
    return (lax.div(a, 64) == b).astype(F32)


def dot(a, b, dims=(((1,), (0,)), ((), ())), precision=None):
    return lax.dot_general(a, b, dims, precision=precision, preferred_element_type=F32)


def doc_of(pos, s1, s2):
    one = jnp.where(pos >= s1, 1, 0) + jnp.where(pos >= s2, 1, 0)
    return jnp.where(pos >= 0, one, -1)


def softplus(z):
    return jnp.maximum(z, 0.0) + jnp.log1p(jnp.exp(-jnp.abs(z)))


def layer(
    q, k, v, x, b, c, dt, conv_x, conv_b, conv_c, bias, rate, skip, gain, windows, lens,
    ao, mo, asum, msum,
    qo, kvo, xo, bo, co, dto, txo, tbo, tco, xs, bs, cs,
    base_o, inflow_o, cc_o, part_o, decay_o, send, got, back, inc,
    scores, top, acc, tot, low_o, qs, att, mam, sums,
    buf_y, buf_x, buf_f, send_x, send_f,
    sq, rq, sx, rx, st, rt, sg, rg, sf, rf, s1, r1, s2, r2, sa, ra, sm, rm, sc, ry, rxx, rff,
):
    X, Y, Z, H, C = coords()
    s = X * 4 + Y
    T = H * 2 + C
    u = Z * 4 + T
    zz = H * 4 + Z
    half = lax.div(Z, 2)
    bar = pltpu.get_barrier_semaphore()

    def signal(**where):
        pl.semaphore_signal(bar, 1, device_id=where, device_id_type=MESH_ID)

    def remote(src, dst, ssem, rsem, where):
        return pltpu.make_async_remote_copy(
            src, dst, ssem, rsem, device_id=where, device_id_type=MESH_ID)

    def at(super_index):
        n = lax.rem(super_index + 16, 16)
        return {"X": lax.div(n, 4), "Y": lax.rem(n, 4)}

    def chip(o):
        n = lax.rem(zz + o, 8)
        return lax.div(n, 4), lax.rem(n, 4)

    order8 = (4, 3, 5, 2, 6, 1, 7)
    order16 = [(o, e) for o in order8 for e in (0, 1)] + [(0, 1)]

    for o, e in order16:
        zh, zl = chip(o)
        signal(zl=zl, zh=zh, c=lax.rem(C + e, 2))
    for d in range(1, 16):
        signal(**at(s + d))

    @pl.when(jnp.logical_and(C == 0, s >= 9))
    def _():
        signal(**at(s - 9), c=1)
    signal(**at(s - 1), zl=3, zh=1, c=1)

    kvo[0:128, :] = jnp.zeros((128, 256), BF)
    kvo[4864:5120, :] = jnp.zeros((256, 256), BF)
    expected = 30 + jnp.where(jnp.logical_and(C == 1, s <= 6), 1, 0) + jnp.where(u == 15, 16, 0)
    pl.semaphore_wait(bar, expected)

    srow = lax.rem(Z, 2) * 128 + T * 32
    slot = lax.rem(Z, 2) * 4 + T

    def qkv_parts(o):
        zh, zl = chip(o)
        g = zh * 4 + zl
        krow = BACK + half * 256 + srow
        k_dst = kvo.at[pl.ds(aligned(krow, 32), 32), 0:128]
        v_dst = kvo.at[pl.ds(aligned(krow, 32), 32), 128:256]
        q_dst = qo.at[pl.ds(aligned(srow, 32), 32), :]
        k_src = k.at[:, pl.ds(aligned(g * 128, 128), 128)]
        v_src = v.at[:, pl.ds(aligned(g * 128, 128), 128)]
        q_src = q.at[:, pl.ds(aligned(g * 512, 512), 512)]
        return {"zh": zh, "zl": zl, "c": half}, ((k_src, k_dst), (v_src, v_dst), (q_src, q_dst))

    def qkv_copy(o, i):
        where, parts = qkv_parts(o)
        src, dst = parts[i]
        return remote(src, dst, sq.at[i, o], rq.at[i, slot], where)

    def qkv_start(kinds):
        for o in order8:
            for i in kinds:
                qkv_copy(o, i).start()

        @pl.when(half != C)
        def _():
            for i in kinds:
                qkv_copy(0, i).start()

        @pl.when(half == C)
        def _():
            parts = qkv_parts(0)[1]
            for i in kinds:
                src, dst = parts[i]
                dst[...] = src[...]

    def columns(o, e):
        zh, zl = chip(o)
        cc = lax.rem(C + e, 2)
        tensor = zh * 2 + cc
        xcol = tensor * 2048 + zl * 512
        gcol = (tensor * 2 + lax.div(zl, 2)) * 128
        wide = pl.ds(aligned(xcol, 512), 512)
        thin = pl.ds(aligned(gcol, 128), 128)
        return {"zh": zh, "zl": zl, "c": cc}, wide, thin

    def col_parts(o, e):
        where, wide, thin = columns(o, e)
        rows = pl.ds(aligned(u * 32, 32), 32)
        return where, (
            (dt, dto.at[rows, :]),
            (b.at[:, thin], bo.at[rows, :]),
            (c.at[:, thin], co.at[rows, :]),
            (x.at[:, wide], xo.at[rows, :]),
        )

    def col_copy(o, e, i):
        where, parts = col_parts(o, e)
        src, dst = parts[i]
        return remote(src, dst, sx.at[i, o * 2 + e], rx.at[i, u], where)

    def tail_copy(o, e, i):
        where, wide, thin = columns(o, e)
        src, dst, col = ((x, txo, wide), (b, tbo, thin), (c, tco, thin))[i]
        return remote(src.at[16:32, col], dst, st.at[i, o * 2 + e], rt.at[i], {**at(s + 1), **where})

    qkv_start((0, 1))
    for i in range(4):
        for o, e in order16:
            col_copy(o, e, i).start()
    for i, (src, dst) in enumerate(col_parts(0, 0)[1]):
        dst[...] = src[...]

    @pl.when(u == 15)
    def _():
        for o in range(8):
            for e in (0, 1):
                for i in range(3):
                    tail_copy(o, e, i).start()
    qkv_start((2,))

    def qkv_landed(i):
        for j in range(2):
            for t in range(4):
                row = j * 128 + t * 32
                if i == 2:
                    dst = qo.at[row:row + 32, :]
                else:
                    krow = aligned(BACK + C * 256 + row, 32)
                    dst = kvo.at[pl.ds(krow, 32), i * 128:i * 128 + 128]

                @pl.when(jnp.logical_or(2 * C + j != Z, T != t))
                def _():
                    landed(dst, rq.at[i, j * 4 + t])

    qkv_landed(0)
    qkv_landed(1)

    def half_rows(d):
        return kvo.at[pl.ds(aligned(BACK - SUPER * d + C * 256, 256), 256), :]

    def partner_rows(d):
        return kvo.at[pl.ds(aligned(BACK - SUPER * d + (1 - C) * 256, 256), 256), :]

    def pass_on(d):
        return remote(half_rows(0), half_rows(d), sg.at[d], rg.at[d], at(s + d))

    def pass_last():
        return remote(kvo.at[BACK + 384:BACK + 512, :], kvo.at[128:256, :], sg.at[9], rg.at[9],
                      {**at(s + 9), "c": 0})

    def to_partner(d):
        return remote(half_rows(d), half_rows(d), sf.at[d], rf.at[d], {"c": 1 - C})

    last_out = jnp.logical_and(C == 1, s <= 6)
    for d in range(1, 9):
        @pl.when(s + d < 16)
        def _():
            pass_on(d).start()

    @pl.when(last_out)
    def _():
        pass_last().start()
    to_partner(0).start()

    def forward(d):
        @pl.when(s >= d)
        def _():
            landed(half_rows(d), rg.at[d])
            to_partner(d).start()

    for i in range(4):
        for o, e in order16:
            zs = lax.rem(zz + 8 - o, 8)
            us = lax.rem(zs, 4) * 4 + lax.div(zs, 4) * 2 + lax.rem(C + e, 2)
            dst = (dto, bo, co, xo)[i].at[pl.ds(aligned(us * 32, 32), 32), :]
            landed(dst, rx.at[i, us])
    for i in range(3):
        landed((txo, tbo, tco)[i], rt.at[i])

    st1 = lens[0]
    st2 = lens[0] + lens[1]
    p0 = s * SUPER
    own = (lax.broadcasted_iota(jnp.int32, (8, 32), 1)
           == lax.broadcasted_iota(jnp.int32, (8, 32), 0) + 8 * Z)

    def column(ref):
        return jnp.sum(jnp.where(own, ref[...], 0.0), axis=1, keepdims=True)

    pick32 = (lax.broadcasted_iota(jnp.int32, (32, 8), 0)
              == lax.broadcasted_iota(jnp.int32, (32, 8), 1) + 8 * Z).astype(F32)

    def row(ref):
        return dot(ref[...], pick32, precision=HIGH)

    first_head = T * 32 + Z * 8
    pick = (lax.broadcasted_iota(jnp.int32, (128, 8), 0)
            == lax.broadcasted_iota(jnp.int32, (128, 8), 1) + first_head).astype(BF)
    dcol = softplus(dot(dto[...], pick) + row(bias))
    drow = softplus(dot(pick, dto[...], (((0,), (1,)), ((), ()))) + column(bias))
    lcol = -dcol * row(rate)
    lrow = -drow * column(rate)
    wide = spread_matrix(8, 512)
    tall = spread_matrix(512, 8)
    skip_wide = dot(row(skip), wide, precision=HIGH)

    for src, tail, buf in ((xo, txo, xs), (bo, tbo, bs), (co, tco, cs)):
        buf[0:16, :] = tail[...].astype(F32)
        buf[16:528, :] = src[...].astype(F32)
    taps_x = conv_x[:, pl.ds(aligned(Z * 512, 512), 512)].astype(F32)
    group = pl.ds(aligned(half * 128, 128), 128)
    taps_b = conv_b[:, group].astype(F32)
    taps_c = conv_c[:, group].astype(F32)

    ti = lax.broadcasted_iota(jnp.int32, (128, 128), 0)
    si = lax.broadcasted_iota(jnp.int32, (128, 128), 1)
    lower = (ti >= si).astype(F32)
    upper = (ti <= si).astype(F32)
    state = jnp.zeros((512, 128), F32)
    decay = jnp.ones((8, 128), F32)
    for n in range(4):
        part_o[n] = state
        decay_o[n] = decay
        pb = p0 + n * 128
        rows = slice(n * 128, n * 128 + 128)
        pcol = pb + lax.broadcasted_iota(jnp.int32, (128, 1), 0)
        prow = pb + lax.broadcasted_iota(jnp.int32, (1, 128), 1)
        start = jnp.where(pcol >= st2, st2, jnp.where(pcol >= st1, st1, 0))
        keep = [pcol - j >= start for j in range(4)]

        def conv(buf, taps):
            total = None
            for j in range(4):
                lo = 16 + n * 128 - j
                term = taps[j:j + 1, :] * buf[lo:lo + 128, :]
                if j:
                    term = jnp.where(keep[j], term, 0.0)
                total = term if total is None else total + term
            return (total / (1.0 + jnp.exp(-total))).astype(BF)

        xc = conv(xs, taps_x)
        bc = conv(bs, taps_b)
        cc = conv(cs, taps_c)
        cc_o[rows, :] = cc
        ccol = dot(lower, lcol[rows, :], precision=HIGH)
        crow = dot(lrow[:, rows], upper, precision=HIGH)
        doc_c = doc_of(pcol, st1, st2)
        doc_r = doc_of(prow, st1, st2)
        allowed = jnp.logical_and(ti >= si, doc_c == doc_r)
        cross = jnp.where(allowed, dot(cc, bc, NT), 0.0)
        xf = xc.astype(F32)
        for pair in range(4):
            mixes = []
            for h in (2 * pair, 2 * pair + 1):
                gap = ccol[:, h:h + 1] - crow[h:h + 1, :]
                seg = jnp.exp(jnp.minimum(gap, 0.0))
                mixes.append((seg * cross * drow[h:h + 1, rows]).astype(BF))
            xp = xc[:, pair * 128:pair * 128 + 128]
            zero = jnp.zeros_like(xp)
            both = jnp.concatenate(
                [jnp.where(si < 64, xp, zero), jnp.where(si < 64, zero, xp)], axis=0)
            intra = dot(jnp.concatenate(mixes, axis=1), both)
            cols = slice(pair * 128, pair * 128 + 128)
            base_o[rows, cols] = intra + skip_wide[:, cols] * xf[:, cols]
        doc_e = doc_of(pb + 127, st1, st2)
        doc_p = doc_of(pb - 1, st1, st2)
        to_end = jnp.where(doc_c == doc_e, jnp.exp(ccol[127:128, :] - ccol), 0.0) * dcol[rows, :]
        weighted = (dot(to_end, wide, precision=HIGH) * xf).astype(BF)
        factor = jnp.where(doc_p == doc_e, jnp.exp(crow[:, 127:128]), 0.0)
        factor = jnp.broadcast_to(factor, (8, 128))
        inflow_o[rows, :] = jnp.where(doc_c == doc_p, jnp.exp(ccol), 0.0)
        state = dot(tall, factor, precision=HIGH) * state + dot(weighted, bc, TN)
        decay = factor * decay
        forward(2 * n + 1)
        forward(2 * n + 2)
    for j in range(16):
        send[j, 0:32, :] = state[j * 32:j * 32 + 32, :]
        send[j, 32:40, :] = jnp.broadcast_to(decay[j // 2:j // 2 + 1, :], (8, 128))

    def peer(d):
        n = lax.rem(s + d, 16)
        return n, {"X": lax.div(n, 4), "Y": lax.rem(n, 4)}

    def there(d):
        n, where = peer(d)
        return remote(send.at[n], got.at[s], s1.at[d], r1.at[s], where)

    inc_rows = pl.ds(aligned(s * 32, 32), 32)

    def again(d):
        n, where = peer(d)
        return remote(back.at[n], inc.at[inc_rows, :], s2.at[d], r2.at[s], where)

    qkv_landed(2)
    t0 = s * SUPER + C * 256
    first = s * SUPER - BACK
    tcol = t0 + lax.broadcasted_iota(jnp.int32, (256, 1), 0)
    start_col = jnp.where(tcol >= st2, st2, jnp.where(tcol >= st1, st1, 0))
    for h in range(4):
        w = windows[zz * 4 + h]
        low = jnp.maximum(tcol - w + 1, start_col)
        low_o[h * 256:h * 256 + 256, :] = jnp.broadcast_to(low, (256, 128))
        qs[h * 256:h * 256 + 256, :] = qo[:, h * 128:h * 128 + 128]
    for d in range(1, 16):
        there(d).start()
    got[s] = send[s]
    top[...] = jnp.full((1024, 128), NEG_LARGE, F32)
    acc[...] = jnp.zeros((1024, 128), F32)
    tot[...] = jnp.zeros((1024, 128), F32)

    @pl.when(jnp.logical_and(C == 0, s >= 9))
    def _():
        landed(kvo.at[128:256, :], rg.at[9])
    landed(partner_rows(0), rf.at[0])
    for d in range(1, 9):
        @pl.when(s >= d)
        def _():
            landed(partner_rows(d), rf.at[d])

    end_row = BACK + C * 256 + 256
    c0 = jnp.maximum(C, 17 - 2 * s)
    count = lax.div(end_row - c0 * 256 + 511, 512)
    lane = lax.broadcasted_iota(jnp.int32, (1, 128), 1)
    trow = t0 + lax.broadcasted_iota(jnp.int32, (256, 128), 0)

    def score_chunk(i, causal):
        r = aligned(c0 * 256 + i * 512, 256)
        keys = kvo[pl.ds(r, 512), 0:128]
        score = dot(qs[...], keys, NT)
        best = None
        for j in range(4):
            part = score[:, j * 128:j * 128 + 128]
            kpos = first + r + j * 128 + lane
            ok = kpos >= low_o[...]
            if causal:
                ok = jnp.logical_and(ok, jnp.concatenate([kpos <= trow] * 4, axis=0))
            part = jnp.where(ok, part, NEG_LARGE)
            scores[:, pl.ds(aligned(i * 512 + j * 128, 128), 128)] = part
            best = part if best is None else jnp.maximum(best, part)
        top[...] = jnp.maximum(top[...], best)

    @pl.loop(0, count - 1)
    def _(i):
        score_chunk(i, False)
    score_chunk(count - 1, True)

    for d in range(1, 16):
        n, _ = peer(16 - d)
        landed(got.at[n], r1.at[n])
    value = jnp.zeros((4, 8, 128), F32)
    for n in range(16):
        back[n] = value.reshape(32, 128).astype(BF)
        value = got[n, 32:40, :][None] * value + got[n, 0:32, :].reshape(4, 8, 128)
    inc[inc_rows, :] = back[s]
    top[...] = jnp.broadcast_to(jnp.max(top[...], axis=1, keepdims=True), (1024, 128))
    for d in range(1, 16):
        again(d).start()

    scale = math.log2(math.e) / math.sqrt(128)

    @pl.loop(0, count)
    def _(i):
        r = aligned(c0 * 256 + i * 512, 256)
        best = top[...]
        weights = [
            jnp.exp2((scores[:, pl.ds(aligned(i * 512 + j * 128, 128), 128)] - best) * scale)
            for j in range(4)
        ]
        tot[...] += (weights[0] + weights[1]) + (weights[2] + weights[3])
        weight = jnp.concatenate([part.astype(BF) for part in weights], axis=1)
        acc[...] += dot(weight, kvo[pl.ds(r, 512), 128:256])

    for h in range(4):
        rows = slice(h * 256, h * 256 + 256)
        total = jnp.sum(tot[rows, :], axis=1, keepdims=True)
        result = (acc[rows, :] / total).astype(BF)
        att[:, h * 128:h * 128 + 128] = result
        sums[4 + h:5 + h, :] = jnp.sum(result.astype(F32), axis=0, keepdims=True)

    def cols_of(block):
        return pl.ds(aligned(block * 512, 512), 512)

    def mam_copy(n):
        return remote(mam.at[pl.ds(aligned(n * 128, 128), 128), :], mo.at[:, cols_of(Z)],
                      sm.at[n], rm.at[Z], {"zl": n})

    def att_copy(j):
        return remote(att.at[j * 128:j * 128 + 128, :], ao.at[:, cols_of(lax.rem(Z, 2))],
                      sa.at[j], ra.at[lax.rem(Z, 2)], {"zl": 2 * C + j, "c": half})

    for d in range(1, 16):
        n, _ = peer(16 - d)
        landed(inc.at[pl.ds(aligned(n * 32, 32), 32), :], r2.at[n])
    for j in range(2):
        mine = jnp.logical_and(2 * C + j == Z, half == C)

        @pl.when(jnp.logical_not(mine))
        def _():
            att_copy(j).start()

        @pl.when(mine)
        def _():
            ao[:, cols_of(lax.rem(Z, 2))] = att[j * 128:j * 128 + 128, :]

    gain_row = gain[:, pl.ds(aligned(Z * 512, 512), 512)]
    average = jnp.where(lax.div(ti, 64) == lax.div(si, 64), 1.0 / 64, 0.0).astype(F32)
    entering = inc[...].astype(F32)
    total = jnp.zeros((1, 512), F32)
    for o in range(4):
        n = lax.rem(Z + 1 + o, 4)
        rows = pl.ds(aligned(n * 128, 128), 128)
        state = (dot(tall, decay_o[n], precision=HIGH) * entering + part_o[n]).astype(BF)
        flow = dot(inflow_o[rows, :], wide, precision=HIGH)
        full = base_o[rows, :] + dot(cc_o[rows, :], state, NT) * flow
        for pair in range(4):
            cols = slice(pair * 128, pair * 128 + 128)
            f = full[:, cols]
            mean = dot(f * f, average, precision=HIGH)
            result = (f * lax.rsqrt(mean + EPS_NORM) * gain_row[:, cols]).astype(BF)
            mam[rows, cols] = result
            sums_part = jnp.sum(result.astype(F32), axis=0, keepdims=True)
            if o == 0:
                sums[pair:pair + 1, :] = sums_part
            else:
                sums[pair:pair + 1, :] += sums_part
        if o:
            mam_copy(lax.rem(Z + o, 4)).start()
    mo[:, cols_of(Z)] = mam[pl.ds(aligned(Z * 128, 128), 128), :]

    def along(name, mine, d, src, buf, recv, base):
        return remote(src, buf.at[mine], sc.at[base + d], recv.at[mine], {name: lax.rem(mine + d, 4)})

    near = [(o, e) for o in range(4) for e in (0, 1) if o or e]
    for d in range(1, 4):
        along("Y", Y, d, sums, buf_y, ry, 0).start()
    buf_y[Y] = sums[...]
    for d in range(1, 4):
        n = lax.rem(Y + d, 4)
        landed(buf_y.at[n], ry.at[n])
    send_x[...] = (buf_y[0] + buf_y[1]) + (buf_y[2] + buf_y[3])
    buf_x[X] = send_x[...]
    for d in range(1, 4):
        along("X", X, d, send_x, buf_x, rxx, 4).start()
    for d in range(1, 4):
        n = lax.rem(X + d, 4)
        landed(buf_x.at[n], rxx.at[n])
    place = Z * 2 + C
    send_f[...] = (buf_x[0] + buf_x[1]) + (buf_x[2] + buf_x[3])
    buf_f[place] = send_f[...]

    def last_copy(o, e):
        return remote(send_f, buf_f.at[place], sc.at[8 + o * 2 + e], rff.at[place],
                      {"zl": lax.rem(Z + o, 4), "c": lax.rem(C + e, 2)})

    for o, e in near:
        last_copy(o, e).start()

    for i in range(3):
        for o in order8:
            qkv_copy(o, i).wait_send()

        @pl.when(half != C)
        def _():
            qkv_copy(0, i).wait_send()
    for i in range(4):
        for o, e in order16:
            col_copy(o, e, i).wait_send()

    @pl.when(u == 15)
    def _():
        for o in range(8):
            for e in (0, 1):
                for i in range(3):
                    tail_copy(o, e, i).wait_send()
    to_partner(0).wait_send()
    for d in range(1, 9):
        @pl.when(s + d < 16)
        def _():
            pass_on(d).wait_send()

        @pl.when(s >= d)
        def _():
            to_partner(d).wait_send()

    @pl.when(last_out)
    def _():
        pass_last().wait_send()
    for d in range(1, 16):
        there(d).wait_send()
        again(d).wait_send()

    for o, e in near:
        n = lax.rem(Z + o, 4) * 2 + lax.rem(C + e, 2)
        landed(buf_f.at[n], rff.at[n])
    for n in range(4):
        msum[n * 4:n * 4 + 4, :] = buf_f[n * 2 + C, 0:4, :]
    for j in range(2):
        spot = (2 * C + j) * 2
        asum[j * 4:j * 4 + 4, :] = buf_f[spot, 4:8, :] + buf_f[spot + 1, 4:8, :]
    for j in range(2):
        @pl.when(jnp.logical_or(2 * C + j != Z, half != C))
        def _():
            landed(ao.at[:, j * 512:j * 512 + 512], ra.at[j])
            att_copy(j).wait_send()
    for d in range(1, 4):
        n = lax.rem(Z + d, 4)
        landed(mo.at[:, cols_of(n)], rm.at[n])
        mam_copy(n).wait_send()
        along("Y", Y, d, sums, buf_y, ry, 0).wait_send()
        along("X", X, d, send_x, buf_x, rxx, 4).wait_send()
    for o, e in near:
        last_copy(o, e).wait_send()


def call_layer(*args):
    dma = pltpu.SemaphoreType.DMA
    shapes = (
        ((256, 512), BF), ((KV_ROWS, 256), BF), ((512, 512), BF), ((512, 128), BF),
        ((512, 128), BF), ((512, 128), BF), ((16, 512), BF), ((16, 128), BF), ((16, 128), BF),
        ((528, 512), F32), ((528, 128), F32), ((528, 128), F32),
        ((512, 512), F32), ((512, 8), F32), ((512, 128), BF), ((4, 512, 128), F32),
        ((4, 8, 128), F32), ((16, 40, 128), F32), ((16, 40, 128), F32), ((16, 32, 128), BF),
        ((512, 128), BF),
        ((1024, 4608), F32), ((1024, 128), F32), ((1024, 128), F32), ((1024, 128), F32),
        ((1024, 128), jnp.int32), ((1024, 128), BF), ((256, 512), BF), ((512, 512), BF),
        ((8, 128), F32),
        ((4, 8, 128), F32), ((4, 8, 128), F32), ((8, 8, 128), F32), ((8, 128), F32),
        ((8, 128), F32),
    )
    sems = ((3, 8), (3, 8), (4, 16), (4, 16), (3, 16), (3,), (10,), (10,), (9,), (9,),
            (16,), (16,), (16,), (16,), (2,), (2,), (4,), (4,), (16,), (4,), (4,), (8,))
    outs = (((128, 1024), BF), ((128, 2048), BF), ((8, 128), F32), ((16, 128), F32))
    return pl.pallas_call(
        layer,
        out_shape=[pltpu.VMEM(n, t) for n, t in outs],
        in_specs=[VM] * 14 + [SM] * 2,
        out_specs=[VM] * 4,
        scratch_shapes=[pltpu.VMEM(n, t) for n, t in shapes] + [dma(n) for n in sems],
        compiler_params=pltpu.CompilerParams(
            collective_id=1, has_side_effects=True, vmem_limit_bytes=56 << 20),
        name="layer",
    )(*args)


def emit(a, b, c, d, ao, bo, co, do, sem):
    copies = [pltpu.make_async_copy(src, dst, sem.at[i])
              for i, (src, dst) in enumerate(((a, ao), (b, bo), (c, co), (d, do)))]
    for copy in copies:
        copy.start()
    for copy in copies:
        copy.wait()


def call_emit(*args):
    return pl.pallas_call(
        emit,
        out_shape=[jax.ShapeDtypeStruct(a.shape, a.dtype) for a in args],
        in_specs=[VM] * 4,
        out_specs=[pl.BlockSpec(memory_space=pl.ANY)] * 4,
        scratch_shapes=[pltpu.SemaphoreType.DMA((4,))],
        name="emit",
    )(*args)


def local(
    queries, keys, values, mamba_x, mamba_b, mamba_c, mamba_dt, conv_x, conv_b, conv_c,
    dt_bias, decay_rate, skip_gain, norm_gain, windows, doc_lengths,
):
    results = call_layer(
        queries, keys, values, mamba_x, mamba_b, mamba_c, mamba_dt, conv_x, conv_b, conv_c,
        dt_bias.reshape(1, 32), decay_rate.reshape(1, 32), skip_gain.reshape(1, 32),
        norm_gain.reshape(1, 2048), windows, doc_lengths)
    ao, mo, asum, msum = results
    return ao, mo, asum.reshape(1024), msum.reshape(2048)


def solution(mesh):
    torus = Mesh(mesh.devices.reshape(4, 4, 4, 2, 2), AXES)
    tokens = P(AXES, None)
    tensor = ("zh", "c")
    in_specs = (tokens,) * 7 + (P(None, tensor),) * 3 + (P(tensor),) * 4 + (P(), P())
    out_specs = (P(("X", "Y", "zl"), tensor), P(("X", "Y", "zl"), tensor), P(tensor), P(tensor))
    return jax.shard_map(local, mesh=torus, in_specs=in_specs, out_specs=out_specs, check_vma=False)
```

time: 127 us -> 87.3 us (0.69); the launches traced: 125 us -> 87.2 us
  Pallas kernels: 118 us -> 83.9 us
  local copies, waits for them, and re-layouts: 6.12 us -> 2.69 us
    pallas_call x6 -> x1, Pallas kernels: 118 us -> 83.9 us  [call_layer(): pl.pallas_call(layer, out_shape=[pltpu.VMEM(n, t) for n, t in outs], in_s...]
    unnamed x4, local copies, waits for them, and re-layouts: 6.12 us -> 2.69 us
where the time goes in v2:
time: 87.3 us; the launch traced here: 87.2 us
  Pallas kernels  83.9 us (96%)
  local copies, waits for them, and re-layouts  2.69 us (3%)
    pallas_call x1, Pallas kernels, call_layer(): pl.pallas_call(layer, out_shape=[pltpu.VMEM(n, t) for n, t in outs], in_s...  83.9 us
    unnamed x4, local copies, waits for them, and re-layouts  2.69 us

profile of v2, /device:TPU:1, one launch (start us, length us, event | category | flops | bytes accessed | tf_op | source)
XLA Modules:
  0.0 87.2 jit_solution(5899848613360202145)
XLA Ops:
  0.6 83.9 %layer.1 = (bf16[128,1024]{1,0:T(8,128)(2,1)S(1)}, bf16[128,2048]{1,0:T(8,128)(2,1)S(1)}, f32[8,128]{1,0:T(8,128)S(1)}, f32[16,128]{1,0:T(8,128)S(1)}) custom-call(bf16[32,4096]{1,0:T(8,128)(2,1)} %q.1, bf16[32,1024]{1,0:T(8,128)(2,1)} %k.1, bf16[32,1024]{1,0:T(8,128)(2,1)} %v.1, bf16[32,8192]{1,0:T(8,128)(2,1)} %x.1, bf16[32,1024]{1,0:T(8,128)(2,1)} %b.1, ...), custom_call_target="tpu_custom_call" | custom-call | tf_op jit(solution)/shard_map/layer/pallas_call | solution.py:604
  84.6 0.7 copy.24
  85.3 0.6 copy.26
  85.9 0.6 copy.27
  86.5 0.8 copy.25
